TPU v7x, 32 devices: a whole 2x2x4 slice. The times are simulated.
32 devices in a mesh: expert: 8 (over z, x), dp: 4 (over y, core).
Axes of the slice: x: 2, y: 2, z: 4, core: 2. Of those that a mesh axis runs over, the one named last changes fastest.
Arguments:
- tokens: bfloat16 [4096, 2048], P(('expert', 'dp')), may hold values from -6 to 6
- expert_ids: int32 [4096, 2], P(('expert', 'dp')), may hold values from 0 to 7, all different within a row; in each aligned block of 128 rows (0 to 127, 128 to 255, ...) at most 48 rows name the same one
- gate_scores: float32 [4096, 2], P(('expert', 'dp')), may hold values from 0.2 to 1
- gate_proj: bfloat16 [8, 768, 2048], P('expert', 'dp'), may hold values from -0.125 to 0.125
- up_proj: bfloat16 [8, 768, 2048], P('expert', 'dp'), may hold values from -0.125 to 0.125
- down_proj: bfloat16 [8, 768, 2048], P('expert', 'dp'), may hold values from -0.21875 to 0.21875
- out_grad: bfloat16 [4096, 2048], P(('expert', 'dp')), may hold values from -0.59765625 to 0.59765625
Outputs:
- output: bfloat16 [4096, 2048], P(('expert', 'dp'))
- d_tokens: bfloat16 [4096, 2048], P(('expert', 'dp'))
- d_scores: float32 [4096, 2], P(('expert', 'dp'))
- d_gate_proj: bfloat16 [8, 768, 2048], P('expert', 'dp')
- d_up_proj: bfloat16 [8, 768, 2048], P('expert', 'dp')
- d_down_proj: bfloat16 [8, 768, 2048], P('expert', 'dp')
Inputs may be any that keep to these rules, and one draw needn't show every extreme that they name: `expert_ids`: each token names 2 different experts. Among the routes of one device's 128 tokens no expert is named more than 48 times, and in some devices' blocks some expert is named exactly 48 times.
All inputs are finite; a program needn't handle non-finite values.
Results may differ from a plain program's by a relative error of at most 0.014.
Values may be sent and summed in bfloat16 or wider, within the bound.
No kernel may reach another device: no remote copies, remote signals or barrier semaphores. Data moves between devices by JAX's collectives and lax.ppermute only.
A program may use at most 128 MiB of HBM per device.

v0:
```python
import jax
import jax.numpy as jnp
from jax import lax
from jax.sharding import PartitionSpec as P


def silu_parts(preact):
    logistic = jax.nn.sigmoid(preact)
    return (preact * logistic, logistic * (1.0 + preact * (1.0 - logistic)))


def scatter_slots(values, target, slot_total):
    return jnp.zeros((slot_total, values.shape[1]), values.dtype).at[target].set(values)


def shards(tokens, expert_ids, gate_scores, gate_proj, up_proj, down_proj, out_grad):
    tok_count, model_width = tokens.shape
    routes_per = expert_ids.shape[1]
    experts = lax.axis_size("expert")
    capacity = max(2, 3 * tok_count * routes_per // (2 * experts))
    slot_total = experts * capacity
    flat_ids = expert_ids.reshape(-1)
    onehot = (flat_ids[:, None] == jnp.arange(experts, dtype=jnp.int32)[None, :]).astype(jnp.int32)
    position = jnp.sum(jnp.cumsum(onehot, axis=0) * onehot, axis=1) - 1
    target = flat_ids * capacity + position
    outgoing = scatter_slots(jnp.repeat(tokens, routes_per, axis=0), target, slot_total)
    received = lax.all_to_all(
        outgoing.reshape(experts, capacity, model_width),
        "expert",
        split_axis=0,
        concat_axis=0,
        tiled=True,
    )
    received = received.reshape(slot_total, model_width)
    gate_full, up_full, down_full = (
        lax.all_gather(gate_proj, "dp", axis=1, tiled=True),
        lax.all_gather(up_proj, "dp", axis=1, tiled=True),
        lax.all_gather(down_proj, "dp", axis=1, tiled=True),
    )
    gate_w = gate_full[0]
    up_w = up_full[0]
    down_w = down_full[0]
    gate_pre = jnp.dot(received, gate_w.T, preferred_element_type=jnp.float32)
    up_pre = jnp.dot(received, up_w.T, preferred_element_type=jnp.float32)
    activated, silu_slope = silu_parts(gate_pre)
    hidden = (activated * up_pre).astype(jnp.bfloat16)
    expert_out = jnp.dot(hidden, down_w, preferred_element_type=jnp.float32).astype(jnp.bfloat16)
    returned = lax.all_to_all(
        expert_out.reshape(experts, capacity, model_width),
        "expert",
        split_axis=0,
        concat_axis=0,
        tiled=True,
    )
    pair_out = returned.reshape(slot_total, model_width)[target].astype(jnp.float32)
    scores = gate_scores.reshape(-1, 1)
    output = jnp.sum(
        (scores * pair_out).reshape(tok_count, routes_per, model_width), axis=1
    ).astype(jnp.bfloat16)
    pair_grad = jnp.repeat(out_grad, routes_per, axis=0).astype(jnp.float32)
    d_scores = jnp.sum(pair_grad * pair_out, axis=1).reshape(tok_count, routes_per)
    out_cot = (scores * pair_grad).astype(jnp.bfloat16)
    cot_slots = scatter_slots(out_cot, target, slot_total)
    cot_rows = lax.all_to_all(
        cot_slots.reshape(experts, capacity, model_width),
        "expert",
        split_axis=0,
        concat_axis=0,
        tiled=True,
    )
    cot_rows = cot_rows.reshape(slot_total, model_width)
    gate_full, up_full, down_full = (
        lax.all_gather(gate_proj, "dp", axis=1, tiled=True),
        lax.all_gather(up_proj, "dp", axis=1, tiled=True),
        lax.all_gather(down_proj, "dp", axis=1, tiled=True),
    )
    gate_w = gate_full[0]
    up_w = up_full[0]
    down_w = down_full[0]
    hidden_grad = jnp.dot(cot_rows, down_w.T, preferred_element_type=jnp.float32)
    gate_grad = (hidden_grad * up_pre * silu_slope).astype(jnp.bfloat16)
    up_grad = (hidden_grad * activated).astype(jnp.bfloat16)
    input_grad = (
        jnp.dot(gate_grad, gate_w, preferred_element_type=jnp.float32)
        + jnp.dot(up_grad, up_w, preferred_element_type=jnp.float32)
    ).astype(jnp.bfloat16)
    grad_terms = (
        jnp.dot(gate_grad.T, received, preferred_element_type=jnp.float32)[None],
        jnp.dot(up_grad.T, received, preferred_element_type=jnp.float32)[None],
        jnp.dot(hidden.T, cot_rows, preferred_element_type=jnp.float32)[None],
    )
    gate_sum, up_sum, down_sum = (
        lax.psum_scatter(
            grad_terms[0].astype(jnp.bfloat16), "dp", scatter_dimension=1, tiled=True
        ).astype(jnp.float32),
        lax.psum_scatter(
            grad_terms[1].astype(jnp.bfloat16), "dp", scatter_dimension=1, tiled=True
        ).astype(jnp.float32),
        lax.psum_scatter(
            grad_terms[2].astype(jnp.bfloat16), "dp", scatter_dimension=1, tiled=True
        ).astype(jnp.float32),
    )
    gate_out = gate_sum.astype(jnp.bfloat16)
    up_out = up_sum.astype(jnp.bfloat16)
    down_out = down_sum.astype(jnp.bfloat16)
    returned_grad = lax.all_to_all(
        input_grad.reshape(experts, capacity, model_width),
        "expert",
        split_axis=0,
        concat_axis=0,
        tiled=True,
    )
    pair_input = returned_grad.reshape(slot_total, model_width)[target].astype(jnp.float32)
    d_tokens = jnp.sum(pair_input.reshape(tok_count, routes_per, model_width), axis=1).astype(
        jnp.bfloat16
    )
    return (output, d_tokens, d_scores, gate_out, up_out, down_out)


def solution(mesh):
    in_specs = (
        P(("expert", "dp"), None),
        P(("expert", "dp"), None),
        P(("expert", "dp"), None),
        P("expert", "dp", None),
        P("expert", "dp", None),
        P("expert", "dp", None),
        P(("expert", "dp"), None),
    )
    out_specs = (
        P(("expert", "dp"), None),
        P(("expert", "dp"), None),
        P(("expert", "dp"), None),
        P("expert", "dp", None),
        P("expert", "dp", None),
        P("expert", "dp", None),
    )
    return jax.shard_map(shards, mesh=mesh, in_specs=in_specs, out_specs=out_specs, check_vma=False)
```

profile of v0, /device:TPU:0, one launch (start us, length us, event | category | flops | bytes accessed | tf_op | source)
XLA Modules:
  0.0 246.6 jit_solution(15795800877254802796)
XLA Ops:
  7.2 0.0 copy-start.5
  7.2 0.0 copy-start.3
  7.2 0.0 all-gather.8.cloned.1.call-start
  7.2 0.7 all-gather.8.cloned.1.call-update
  7.9 0.0 all-gather.6.cloned.1.call-start
  8.0 0.7 all-gather.6.cloned.1.call-update
  8.7 0.0 copy-done.5
  8.7 0.1 copy.16
  8.8 0.1 eq.29
  8.9 0.1 eq.25
  9.1 0.1 copy.15
  9.2 0.1 mul.69
  9.4 0.6 reduce-window.6
  9.9 0.2 slice_reduce_fusion
  10.2 0.0 copy-done.3
  10.2 2.4 broadcast_in_dim.5
  12.6 2.7 %convert_element_type.82 = f32[256,2048]{1,0:T(8,128)S(1)} reshape(f32[128,2,2048]{2,1,0:T(2,128)} %broadcast_in_dim.5) | data formatting | bytes 4194304 | tf_op jit(solution)/shard_map/convert_element_type | solution.py:60
  15.3 0.1 copy.14
  15.5 0.1 mul.74
  15.6 0.1 fusion.26
  15.7 3.5 %scatter_custom_fusion.1 = bf16[384,2048]{1,0:T(8,128)(2,1)} fusion(s32[256]{0:T(256)S(1)} %bitcast.61, f32[256,2048]{1,0:T(8,128)S(1)} %convert_element_type.82, f32[256]{0:T(256)S(1)} %mul.74, bf16[]{:T(256)} %constant.7.clone.1), kind=kCustom, calls=%fused_computation.32 | custom fusion | flops 1048576 | bytes 3671042 | tf_op jit(solution)/shard_map/scatter | solution.py:13
  19.2 7.4 %all-to-all-start.2 = ((bf16[8,48,2048]{2,1,0:T(8,128)(2,1)}), bf16[8,48,2048]{2,1,0:T(8,128)(2,1)S(1)}, u32[]{:S(2)}, u32[]{:S(2)}) async-start(bf16[8,48,2048]{2,1,0:T(8,128)(2,1)} %bitcast.57), calls=%async_computation.2 | async-start | bytes 3145728 | tf_op jit(solution)/shard_map/all_to_all | solution.py:64
  26.6 0.0 all-gather.4.cloned.1.call-start
  26.7 0.7 all-gather.4.cloned.1.call-update
  27.4 0.6 broadcast_in_dim.4
  28.0 1.2 reshape.150
  29.2 4.2 %scatter_custom_fusion = bf16[384,2048]{1,0:T(8,128)(2,1)} fusion(s32[256]{0:T(256)S(1)} %bitcast.62, bf16[256,2048]{1,0:T(8,128)(2,1)} %reshape.150, bf16[]{:T(256)} %constant.7.clone.1), kind=kCustom, calls=%fused_computation.35 | custom fusion | bytes 1573376 | tf_op jit(solution)/shard_map/scatter | solution.py:13
  33.4 30.2 %all-to-all-done.2 = bf16[8,48,2048]{2,1,0:T(8,128)(2,1)S(1)} async-done(((bf16[8,48,2048]{2,1,0:T(8,128)(2,1)}), bf16[8,48,2048]{2,1,0:T(8,128)(2,1)S(1)}, u32[]{:S(2)}, u32[]{:S(2)}) %all-to-all-start.2) | async-done | bytes 1572896 | tf_op jit(solution)/shard_map/all_to_all | solution.py:64
  63.6 4.3 %all-to-all-start = ((bf16[8,48,2048]{2,1,0:T(8,128)(2,1)}), bf16[8,48,2048]{2,1,0:T(8,128)(2,1)}, u32[]{:S(2)}, u32[]{:S(2)}) async-start(bf16[8,48,2048]{2,1,0:T(8,128)(2,1)} %bitcast.4), calls=%async_computation | async-start | bytes 3145728 | tf_op jit(solution)/shard_map/all_to_all | solution.py:27
  67.9 0.2 reduce-scatter.4.cloned.1.call-start
  68.2 0.0 all-gather.8.cloned.1.call-done
  68.2 4.3 %fusion = f32[384,768]{1,0:T(8,128)} fusion(bf16[384,2048]{1,0:T(8,128)(2,1)S(1)} %bitcast.58, bf16[1,768,2048]{2,1,0:T(8,128)(2,1)} %all-gather.8.cloned.1.call-done), kind=kOutput, calls=%fused_computation.7 | convolution fusion | flops 1207959552 | bytes 5898240 | tf_op jit(solution)/shard_map/dot_general | solution.py:80
  72.5 32.0 %all-to-all-done = bf16[8,48,2048]{2,1,0:T(8,128)(2,1)} async-done(((bf16[8,48,2048]{2,1,0:T(8,128)(2,1)}), bf16[8,48,2048]{2,1,0:T(8,128)(2,1)}, u32[]{:S(2)}, u32[]{:S(2)}) %all-to-all-start) | async-done | bytes 1572896 | tf_op jit(solution)/shard_map/all_to_all | solution.py:27
  104.6 4.8 %fusion.6 = f32[384,768]{1,0:T(8,128)} fusion(bf16[384,2048]{1,0:T(8,128)(2,1)} %bitcast.5, bf16[1,768,2048]{2,1,0:T(8,128)(2,1)} %all-gather.6.cloned.1.call-done), kind=kOutput, calls=%fused_computation.13 | convolution fusion | flops 1207959552 | bytes 5898240 | tf_op jit(solution)/shard_map/dot_general | solution.py:44
  109.4 5.7 %multiply_convert_fusion.2 = (bf16[384,768]{1,0:T(8,128)(2,1)S(1)}, bf16[384,768]{1,0:T(8,128)(2,1)}, bf16[384,768]{1,0:T(8,128)(2,1)S(1)}) fusion(f32[384,768]{1,0:T(8,128)} %fusion, f32[384,768]{1,0:T(8,128)} %fusion.6, bf16[384,2048]{1,0:T(8,128)(2,1)} %bitcast.5, bf16[1,768,2048]{2,1,0:T(8,128)(2,1)} %all-gather.4.cloned.1.call-done), kind=kOutput, calls=%fused_computation.28 | convolution fusion | flops 1212383232 | bytes 8847360 | tf_op jit(solution)/shard_map/dot_general | solution.py:43
  115.1 0.8 copy-done.9
  116.0 4.9 %fusion.12 = bf16[1,768,2048]{2,1,0:T(8,128)(2,1)} fusion(bf16[384,768]{1,0:T(8,128)(2,1)S(1)} %get-tuple-element.12, bf16[384,2048]{1,0:T(8,128)(2,1)} %bitcast.5), kind=kOutput, calls=%fused_computation.20 | convolution fusion | flops 1209532416 | bytes 5308416 | tf_op jit(solution)/shard_map/dot_general | solution.py:88
  120.9 0.0 reduce-scatter.4.cloned.1.call-update
  120.9 0.0 reduce-scatter.6.cloned.1.call-start
  120.9 5.1 %fusion.13 = bf16[1,768,2048]{2,1,0:T(8,128)(2,1)} fusion(bf16[384,768]{1,0:T(8,128)(2,1)} %get-tuple-element.13, bf16[384,2048]{1,0:T(8,128)(2,1)} %bitcast.5), kind=kOutput, calls=%fused_computation.21 | convolution fusion | flops 1209532416 | bytes 5308416 | tf_op jit(solution)/shard_map/dot_general | solution.py:89
  126.0 0.0 reduce-scatter.6.cloned.1.call-update
  126.0 0.0 reduce-scatter.8.cloned.1.call-start
  126.1 0.0 copy-done.11
  126.1 3.5 %fusion.14 = bf16[1,768,2048]{2,1,0:T(8,128)(2,1)} fusion(bf16[384,768]{1,0:T(8,128)(2,1)S(1)} %get-tuple-element.14, bf16[384,2048]{1,0:T(8,128)(2,1)S(1)} %bitcast.59), kind=kOutput, calls=%fused_computation.22 | convolution fusion | flops 1209532416 | bytes 5308416 | tf_op jit(solution)/shard_map/dot_general | solution.py:90
  129.6 0.0 reduce-scatter.8.cloned.1.call-update
  129.6 2.0 copy-done.7
  131.6 3.6 %fusion.17 = bf16[384,2048]{1,0:T(8,128)(2,1)} fusion(bf16[384,768]{1,0:T(8,128)(2,1)} %copy-done.11, bf16[1,768,2048]{2,1,0:T(8,128)(2,1)S(1)} %copy-done.7), kind=kOutput, calls=%fused_computation.23 | convolution fusion | flops 1208745984 | bytes 5308416 | tf_op jit(solution)/shard_map/dot_general | solution.py:47
  135.2 4.2 %all-to-all-start.1 = ((bf16[8,48,2048]{2,1,0:T(8,128)(2,1)}), bf16[8,48,2048]{2,1,0:T(8,128)(2,1)S(1)}, u32[]{:S(2)}, u32[]{:S(2)}) async-start(bf16[8,48,2048]{2,1,0:T(8,128)(2,1)} %bitcast.9), calls=%async_computation.1 | async-start | bytes 3145728 | tf_op jit(solution)/shard_map/all_to_all | solution.py:48
  139.4 3.4 %fusion.4 = f32[384,2048]{1,0:T(8,128)S(1)} fusion(bf16[384,768]{1,0:T(8,128)(2,1)S(1)} %copy-done.12, bf16[1,768,2048]{2,1,0:T(8,128)(2,1)} %all-gather.6.cloned.1.call-done), kind=kOutput, calls=%fused_computation.11 | convolution fusion | flops 1207959552 | bytes 6881280 | tf_op jit(solution)/shard_map/dot_general | solution.py:85
  142.9 2.6 %add_convert_fusion = bf16[384,2048]{1,0:T(8,128)(2,1)} fusion(f32[384,2048]{1,0:T(8,128)S(1)} %fusion.4, bf16[384,768]{1,0:T(8,128)(2,1)S(1)} %copy-done.10, bf16[1,768,2048]{2,1,0:T(8,128)(2,1)S(1)} %copy-done.8), kind=kOutput, calls=%fused_computation.19 | convolution fusion | flops 1209532416 | bytes 8454144 | tf_op jit(solution)/shard_map/dot_general | solution.py:84
  145.5 31.1 %all-to-all-done.1 = bf16[8,48,2048]{2,1,0:T(8,128)(2,1)S(1)} async-done(((bf16[8,48,2048]{2,1,0:T(8,128)(2,1)}), bf16[8,48,2048]{2,1,0:T(8,128)(2,1)S(1)}, u32[]{:S(2)}, u32[]{:S(2)}) %all-to-all-start.1) | async-done | bytes 1572896 | tf_op jit(solution)/shard_map/all_to_all | solution.py:48
  176.7 3.6 %all-to-all-start.3 = ((bf16[8,48,2048]{2,1,0:T(8,128)(2,1)}), bf16[8,48,2048]{2,1,0:T(8,128)(2,1)S(1)}, u32[]{:S(2)}, u32[]{:S(2)}) async-start(bf16[8,48,2048]{2,1,0:T(8,128)(2,1)} %bitcast.60), calls=%async_computation.3 | async-start | bytes 3145728 | tf_op jit(solution)/shard_map/all_to_all | solution.py:106
  180.3 2.4 gather_fusion
  182.7 3.4 %reshape.129 = f32[128,2,2048]{2,1,0:T(2,128)} reshape(bf16[256,2048]{1,0:T(8,128)(2,1)} %gather_fusion) | data formatting | bytes 3145728 | tf_op jit(solution)/shard_map/convert_element_type | solution.py:55
  186.1 31.4 %all-to-all-done.3 = bf16[8,48,2048]{2,1,0:T(8,128)(2,1)S(1)} async-done(((bf16[8,48,2048]{2,1,0:T(8,128)(2,1)}), bf16[8,48,2048]{2,1,0:T(8,128)(2,1)S(1)}, u32[]{:S(2)}, u32[]{:S(2)}) %all-to-all-start.3) | async-done | bytes 1572896 | tf_op jit(solution)/shard_map/all_to_all | solution.py:106
  217.5 2.3 gather_fusion.1
  219.8 2.7 %gather.10 = bf16[128,2,2048]{2,1,0:T(2,128)(2,1)} reshape(bf16[256,2048]{1,0:T(8,128)(2,1)} %gather_fusion.1) | data formatting | bytes 2097152 | tf_op jit(solution)/shard_map/gather | solution.py:113
  222.5 4.6 %reduce_sum.43 = bf16[128,2048]{1,0:T(8,128)(2,1)} reduce(bf16[128,2,2048]{2,1,0:T(2,128)(2,1)} %gather.10, bf16[]{:T(256)} %constant.7.clone.1), dimensions={1}, to_apply=%region_6.7 | reduce | flops 262144 | bytes 1572866 | tf_op jit(solution)/shard_map/reduce_sum | solution.py:114
  227.1 0.0 copy-done.2
  227.1 0.3 multiply_reduce_fusion
  227.4 0.1 reduce_sum.45
  227.5 0.6 copy.19
  228.2 5.6 %multiply_reduce_fusion.1 = bf16[128,2048]{1,0:T(8,128)(2,1)} fusion(f32[128,2,2048]{2,1,0:T(2,128)} %reshape.129, f32[128,2]{1,0:T(8,128)S(1)} %copy.14), kind=kLoop, calls=%fused_computation.26 | loop fusion | flops 786432 | bytes 2622464 | tf_op jit(solution)/shard_map/reduce_sum | solution.py:57
  233.8 6.0 %reduce-scatter.8.cloned.1.call-done = bf16[1,192,2048]{2,1,0:T(8,128)(2,1)} async-done(((bf16[1,768,2048]{2,1,0:T(8,128)(2,1)}), bf16[1,192,2048]{2,1,0:T(8,128)(2,1)}) %reduce-scatter.8.cloned.1.call-update) | async-done | bytes 786448 | tf_op jit(solution)/shard_map/reduce_scatter | solution.py:99
  (29 shorter events, 0.1 us)
Async XLA Ops:
  7.2 1.5 copy-start.5
  7.2 3.0 %copy-start.3 = (bf16[128,2048]{1,0:T(8,128)(2,1)S(1)}, bf16[128,2048]{1,0:T(8,128)(2,1)}, u32[]{:S(2)}) copy-start(bf16[128,2048]{1,0:T(8,128)(2,1)} %param.13) | copy-start | bytes 1572868
  7.2 61.0 %all-gather.8.cloned.1.call-start = ((), (), s32[]{:S(2)}) async-start(), calls=%async_computation.9 | async-start | bytes 3932160 | tf_op jit(solution)/shard_map/all_gather | solution.py:38
  7.9 96.7 %all-gather.6.cloned.1.call-start = ((), (), s32[]{:S(2)}) async-start(), calls=%async_computation.8 | async-start | bytes 3932160 | tf_op jit(solution)/shard_map/all_gather | solution.py:37
  12.6 2.7 %copy-start.6 = (f32[128,2]{0,1:T(2,128)S(1)}, f32[128,2]{0,1:T(2,128)}, u32[]{:S(2)}) copy-start(f32[128,2]{0,1:T(2,128)} %param.9) | copy-start | bytes 3076
  15.3 3.9 %copy-start = (f32[256,2048]{1,0:T(8,128)}, f32[256,2048]{1,0:T(8,128)S(1)}, u32[]{:S(2)}) copy-start(f32[256,2048]{1,0:T(8,128)S(1)} %convert_element_type.82) | copy-start | bytes 6291460
  19.2 8.2 %copy-start.4 = (bf16[128,2048]{1,0:T(8,128)(2,1)S(1)}, bf16[128,2048]{1,0:T(8,128)(2,1)}, u32[]{:S(2)}) copy-start(bf16[128,2048]{1,0:T(8,128)(2,1)} %param.7) | copy-start | bytes 1572868
  19.2 44.4 %all-to-all-start.2 = ((bf16[8,48,2048]{2,1,0:T(8,128)(2,1)}), bf16[8,48,2048]{2,1,0:T(8,128)(2,1)S(1)}, u32[]{:S(2)}, u32[]{:S(2)}) async-start(bf16[8,48,2048]{2,1,0:T(8,128)(2,1)} %bitcast.57), calls=%async_computation.2 | async-start | bytes 3145728 | tf_op jit(solution)/shard_map/all_to_all | solution.py:64
  26.6 82.8 %all-gather.4.cloned.1.call-start = ((), (), s32[]{:S(2)}) async-start(), calls=%async_computation.7 | async-start | bytes 3932160 | tf_op jit(solution)/shard_map/all_gather | solution.py:36
  63.6 40.9 %all-to-all-start = ((bf16[8,48,2048]{2,1,0:T(8,128)(2,1)}), bf16[8,48,2048]{2,1,0:T(8,128)(2,1)}, u32[]{:S(2)}, u32[]{:S(2)}) async-start(bf16[8,48,2048]{2,1,0:T(8,128)(2,1)} %bitcast.4), calls=%async_computation | async-start | bytes 3145728 | tf_op jit(solution)/shard_map/all_to_all | solution.py:27
  67.9 165.8 %reduce-scatter.4.cloned.1.call-start = ((), (), s32[]{:S(2)}) async-start(), calls=%async_computation.10 | async-start | bytes 3932160 | tf_op jit(solution)/shard_map/reduce_scatter | solution.py:93
  115.1 0.8 copy-start.9
  115.1 11.0 %copy-start.11 = (bf16[384,768]{1,0:T(8,128)(2,1)}, bf16[384,768]{1,0:T(8,128)(2,1)S(1)}, u32[]{:S(2)}) copy-start(bf16[384,768]{1,0:T(8,128)(2,1)S(1)} %get-tuple-element.14) | copy-start | bytes 1769476
  120.9 112.9 %reduce-scatter.6.cloned.1.call-start = ((), (), s32[]{:S(2)}) async-start(), calls=%async_computation.11 | async-start | bytes 3932160 | tf_op jit(solution)/shard_map/reduce_scatter | solution.py:96
  126.0 113.7 %reduce-scatter.8.cloned.1.call-start = ((), (), s32[]{:S(2)}) async-start(), calls=%async_computation.12 | async-start | bytes 3932160 | tf_op jit(solution)/shard_map/reduce_scatter | solution.py:99
  129.6 2.0 copy-start.7
  135.2 4.2 %copy-start.12 = (bf16[384,768]{1,0:T(8,128)(2,1)S(1)}, bf16[384,768]{1,0:T(8,128)(2,1)}, u32[]{:S(2)}) copy-start(bf16[384,768]{1,0:T(8,128)(2,1)} %get-tuple-element.13) | copy-start | bytes 1769476
  135.2 41.5 %all-to-all-start.1 = ((bf16[8,48,2048]{2,1,0:T(8,128)(2,1)}), bf16[8,48,2048]{2,1,0:T(8,128)(2,1)S(1)}, u32[]{:S(2)}, u32[]{:S(2)}) async-start(bf16[8,48,2048]{2,1,0:T(8,128)(2,1)} %bitcast.9), calls=%async_computation.1 | async-start | bytes 3145728 | tf_op jit(solution)/shard_map/all_to_all | solution.py:48
  139.4 3.5 %copy-start.8 = (bf16[1,768,2048]{2,1,0:T(8,128)(2,1)S(1)}, bf16[1,768,2048]{2,1,0:T(8,128)(2,1)}, u32[]{:S(2)}) copy-start(bf16[1,768,2048]{2,1,0:T(8,128)(2,1)} %all-gather.4.cloned.1.call-done) | copy-start | bytes 9437188
  139.4 3.5 %copy-start.10 = (bf16[384,768]{1,0:T(8,128)(2,1)S(1)}, bf16[384,768]{1,0:T(8,128)(2,1)}, u32[]{:S(2)}) copy-start(bf16[384,768]{1,0:T(8,128)(2,1)} %copy-done.9) | copy-start | bytes 1769476
  176.7 40.8 %all-to-all-start.3 = ((bf16[8,48,2048]{2,1,0:T(8,128)(2,1)}), bf16[8,48,2048]{2,1,0:T(8,128)(2,1)S(1)}, u32[]{:S(2)}, u32[]{:S(2)}) async-start(bf16[8,48,2048]{2,1,0:T(8,128)(2,1)} %bitcast.60), calls=%async_computation.3 | async-start | bytes 3145728 | tf_op jit(solution)/shard_map/all_to_all | solution.py:106
  219.8 7.3 %copy-start.1 = (f32[256,2048]{1,0:T(8,128)S(1)}, f32[256,2048]{1,0:T(8,128)}, u32[]{:S(2)}) copy-start(f32[256,2048]{1,0:T(8,128)} %copy-done) | copy-start | bytes 6291460
  219.8 7.3 %copy-start.2 = (bf16[256,2048]{1,0:T(8,128)(2,1)S(1)}, bf16[256,2048]{1,0:T(8,128)(2,1)}, u32[]{:S(2)}) copy-start(bf16[256,2048]{1,0:T(8,128)(2,1)} %gather_fusion) | copy-start | bytes 3145732
Sparse Core Ops, SparseCore 0:
  9.6 31.2 all-gather.7
  42.4 28.4 all-gather.5
  72.5 28.4 all-gather.3
  121.0 36.9 reduce-scatter.3
  161.0 37.8 reduce-scatter.5
  201.8 37.8 reduce-scatter.7
where the time goes:
time: 247 us
  waiting for transfers between devices  133 us (54%)
  matrix products  38 us (15%)
  local copies, waits for them, and re-layouts  26.7 us (11%)
  starting transfers between devices  20 us (8%)
  other arithmetic  14.7 us (6%)
  between operations  14.3 us (6%)
    all_to_all x1, waiting for transfers between devices, shards(): lax.all_to_all(outgoing.reshape(experts, capacity, model_width), 'expert'...  32 us
    all_to_all x1, waiting for transfers between devices, shards(): lax.all_to_all(input_grad.reshape(experts, capacity, model_width), 'exper...  31.4 us
    all_to_all x1, waiting for transfers between devices, shards(): lax.all_to_all(expert_out.reshape(experts, capacity, model_width), 'exper...  31.1 us
    all_to_all x1, waiting for transfers between devices, shards(): lax.all_to_all(cot_slots.reshape(experts, capacity, model_width), 'expert...  30.2 us
    all_to_all x1, starting transfers between devices, shards(): lax.all_to_all(cot_slots.reshape(experts, capacity, model_width), 'expert...  7.41 us
    reduce_scatter x1, waiting for transfers between devices, shards(): lax.psum_scatter(grad_terms[2].astype(jnp.bfloat16), 'dp', scatter_dimens...  6 us
    dot_general x1, matrix products, shards(): gate_pre = jnp.dot(received, gate_w.T, preferred_element_type=jnp.float32)  5.72 us
    reduce_sum x1, other arithmetic, shards(): jnp.sum((scores * pair_out).reshape(tok_count, routes_per, model_width),...  5.59 us
  transfers between devices with their start and end apart: 10, of which 5 were waited for; matrix products, arithmetic and copies ran while one was open for 27% of the time, Pallas kernels for 0%

commit v1 on v0

v1 whole, which is shorter than its diff:
```python
import functools

import jax
import jax.numpy as jnp
from jax import lax
from jax.experimental import pallas as pl
from jax.experimental.pallas import tpu as pltpu
from jax.sharding import PartitionSpec as P


F32 = jnp.float32
BF16 = jnp.bfloat16
VMEM = pl.BlockSpec(memory_space=pltpu.VMEM)
SMEM = pl.BlockSpec(memory_space=pltpu.SMEM)


def silu_parts(preact):
    logistic = jax.nn.sigmoid(preact)
    return (preact * logistic, logistic * (1.0 + preact * (1.0 - logistic)))


def col_tiles(width, step=512):
    step = min(width, step)
    return [slice(n, min(n + step, width)) for n in range(0, width, step)]


def slot_rows(ids_ref, me, experts, capacity):
    routes, toks = ids_ref.shape
    rows = lax.broadcasted_iota(jnp.int32, (experts, toks), 0)
    earlier = (
        lax.broadcasted_iota(jnp.int32, (toks, toks), 0)
        < lax.broadcasted_iota(jnp.int32, (toks, toks), 1)
    ).astype(BF16)
    base = jnp.zeros((experts, 1), F32)
    slots = []
    for k in range(routes):
        rel = ids_ref[k : k + 1, :] ^ me
        named = (rows == rel).astype(F32)
        before = jnp.dot(named.astype(BF16), earlier, preferred_element_type=F32) + base
        base = base + jnp.sum(named, axis=1, keepdims=True)
        place = jnp.sum(before * named, axis=0, keepdims=True)
        slots.append(rel * capacity + place.astype(jnp.int32))
    return slots


def pick(slot, slot_total):
    toks = slot.shape[1]
    return lax.broadcasted_iota(jnp.int32, (slot_total, toks), 0) == slot


def store_chunks(refs, cols, value):
    rows = refs[0].shape[0]
    for r, ref in enumerate(refs):
        ref[:, cols] = value[r * rows : (r + 1) * rows]


def send_tokens_kernel(experts, capacity, me_ref, ids_ref, tokens_ref, slots_ref, *chunk_refs):
    slots = slot_rows(ids_ref, me_ref[0], experts, capacity)
    chosen = None
    for k, slot in enumerate(slots):
        slots_ref[k : k + 1, :] = slot
        hit = pick(slot, experts * capacity)
        chosen = hit if chosen is None else chosen | hit
    chosen = chosen.astype(F32).astype(BF16)
    for cols in col_tiles(tokens_ref.shape[1]):
        rows = jnp.dot(chosen, tokens_ref[:, cols], preferred_element_type=F32)
        store_chunks(chunk_refs, cols, rows.astype(BF16))


def send_cots_kernel(experts, capacity, slots_ref, scores_ref, grad_ref, *chunk_refs):
    chosen, weight = None, None
    for k in range(slots_ref.shape[0]):
        hit = pick(slots_ref[k : k + 1, :], experts * capacity)
        scaled = jnp.where(hit, scores_ref[k : k + 1, :], 0.0)
        chosen = hit if chosen is None else chosen | hit
        weight = scaled if weight is None else weight + scaled
    weight = jnp.sum(weight, axis=1, keepdims=True)
    chosen = chosen.astype(F32).astype(BF16)
    for cols in col_tiles(grad_ref.shape[1]):
        rows = jnp.dot(chosen, grad_ref[:, cols], preferred_element_type=F32)
        store_chunks(chunk_refs, cols, (rows * weight).astype(BF16))


def gather_rows(hit, rows):
    return lax.dot_general(hit, rows, (((0,), (0,)), ((), ())), preferred_element_type=F32)


def dot_nt(left, right):
    return lax.dot_general(left, right, (((1,), (1,)), ((), ())), preferred_element_type=F32)


def load_rows(chunk_refs, rows_ref):
    rows = chunk_refs[0].shape[0]
    for r, ref in enumerate(chunk_refs):
        rows_ref[r * rows : (r + 1) * rows, :] = ref[...]


def load_chunks(refs, cols):
    return jnp.concatenate([ref[:, cols] for ref in refs], axis=0)


def combine_out_kernel(slot_total, slots_ref, scores_ref, grad_ref, *refs):
    *chunk_refs, out_ref, dscore_ref = refs
    routes = slots_ref.shape[0]
    hits = [pick(slots_ref[k : k + 1, :], slot_total).astype(F32).astype(BF16) for k in range(routes)]
    dots = [jnp.zeros((grad_ref.shape[0], 1), F32) for _ in range(routes)]
    for cols in col_tiles(grad_ref.shape[1]):
        rows = load_chunks(chunk_refs, cols)
        grad = grad_ref[:, cols].astype(F32)
        total = None
        for k in range(routes):
            pair = gather_rows(hits[k], rows)
            dots[k] = dots[k] + jnp.sum(pair * grad, axis=1, keepdims=True)
            term = scores_ref[:, k : k + 1] * pair
            total = term if total is None else total + term
        out_ref[:, cols] = total.astype(BF16)
    for k in range(routes):
        dscore_ref[:, k : k + 1] = dots[k]


def combine_grad_kernel(slot_total, slots_ref, *refs):
    *chunk_refs, out_ref = refs
    chosen = None
    for k in range(slots_ref.shape[0]):
        hit = pick(slots_ref[k : k + 1, :], slot_total)
        chosen = hit if chosen is None else chosen | hit
    chosen = chosen.astype(F32).astype(BF16)
    for cols in col_tiles(out_ref.shape[1]):
        out_ref[:, cols] = gather_rows(chosen, load_chunks(chunk_refs, cols)).astype(BF16)


def expert_in_kernel(gate_ref, up_ref, *refs):
    *chunk_refs, rows_ref, hidden_ref, act_ref, slope_ref = refs
    load_rows(chunk_refs, rows_ref)
    rows = rows_ref[...]
    for cols in col_tiles(hidden_ref.shape[1], 256):
        gate_pre = dot_nt(rows, gate_ref[cols, :])
        up_pre = dot_nt(rows, up_ref[cols, :])
        activated, slope = silu_parts(gate_pre)
        hidden_ref[:, cols] = (activated * up_pre).astype(BF16)
        act_ref[:, cols] = activated
        slope_ref[:, cols] = slope * up_pre


def expert_out_kernel(hidden_ref, down_ref, *chunk_refs):
    hidden = hidden_ref[...]
    for cols in col_tiles(down_ref.shape[1]):
        store_chunks(chunk_refs, cols, jnp.dot(hidden, down_ref[:, cols], preferred_element_type=F32).astype(BF16))


def hidden_grad_kernel(down_ref, act_ref, slope_ref, cots_ref, gate_grad_ref, up_grad_ref):
    cots = cots_ref[...]
    for cols in col_tiles(act_ref.shape[1], 256):
        hidden_grad = dot_nt(cots, down_ref[cols, :])
        gate_grad_ref[:, cols] = (hidden_grad * slope_ref[:, cols]).astype(BF16)
        up_grad_ref[:, cols] = (hidden_grad * act_ref[:, cols]).astype(BF16)


def input_grad_kernel(gate_grad_ref, up_grad_ref, gate_ref, up_ref, *chunk_refs):
    gate_grad, up_grad = gate_grad_ref[...], up_grad_ref[...]
    for cols in col_tiles(gate_ref.shape[1]):
        total = jnp.dot(gate_grad, gate_ref[:, cols], preferred_element_type=F32)
        total = total + jnp.dot(up_grad, up_ref[:, cols], preferred_element_type=F32)
        store_chunks(chunk_refs, cols, total.astype(BF16))


def weight_grad_kernel(left_ref, right_ref, *part_refs):
    step = part_refs[0].shape[0]
    per = 2 if len(part_refs) % 2 == 0 else len(part_refs)
    for first in range(0, len(part_refs), per):
        left = left_ref[:, first * step : (first + per) * step]
        for cols in col_tiles(right_ref.shape[1]):
            store_chunks(part_refs[first : first + per], cols, gather_rows(left, right_ref[:, cols]).astype(BF16))


def join_kernel(*refs):
    *chunk_refs, rows_ref = refs
    load_rows(chunk_refs, rows_ref)


def add_kernel(*refs):
    *term_refs, out_ref = refs
    total = term_refs[0][...].astype(F32)
    for ref in term_refs[1:]:
        total = total + ref[...].astype(F32)
    out_ref[...] = total.astype(BF16)


def add(terms):
    return call(add_kernel, terms, jax.ShapeDtypeStruct(terms[0].shape, BF16))


def call(kernel, args, shapes, flops=0):
    single = not isinstance(shapes, list)
    return pl.pallas_call(
        kernel,
        out_shape=shapes,
        in_specs=[SMEM if a.ndim == 1 else VMEM for a in args],
        out_specs=VMEM if single else [VMEM] * len(shapes),
        cost_estimate=pl.CostEstimate(flops=flops, transcendentals=0, bytes_accessed=0),
        compiler_params=pltpu.CompilerParams(vmem_limit_bytes=24 * 1024 * 1024),
    )(*args)


def swap(value, axis, size, bits):
    return lax.ppermute(value, axis, [(i, i ^ bits) for i in range(size)])


def exchange(chunks, size):
    if len(chunks) == 1:
        rows, width = chunks[0].shape
        moved = lax.all_to_all(
            chunks[0].reshape(size, rows // size, width), "expert", split_axis=0, concat_axis=0, tiled=True
        )
        return [moved.reshape(rows, width)]
    got = {0: chunks[0]}
    for j in sorted(range(1, size), reverse=True):
        got[j] = swap(chunks[j], "expert", size, j)
    return [got[j] for j in range(size)]


def gather_shards(shard, size):
    have = {0: shard}
    bit = size // 2
    while bit:
        for j in list(have):
            have[j ^ bit] = swap(have[j], "dp", size, bit)
        bit //= 2
    return call(join_kernel, [have[j] for j in range(size)], jax.ShapeDtypeStruct((size * shard.shape[0], shard.shape[1]), BF16))


def scatter_sum(parts, size):
    terms = {j: [part] for j, part in enumerate(parts)}
    bit = 1
    while bit < size:
        for j in sorted((j for j in terms if j & bit), reverse=True):
            sent = terms.pop(j)
            sent = sent[0] if len(sent) == 1 else add(sent)
            terms[j ^ bit].append(swap(sent, "dp", size, bit))
        bit *= 2
    return add(terms[0])


def body(tokens, expert_ids, gate_scores, gate_proj, up_proj, down_proj, out_grad):
    tok_count, width = tokens.shape
    routes = expert_ids.shape[1]
    experts = lax.axis_size("expert")
    n_dp = lax.axis_size("dp")
    capacity = max(2, 3 * tok_count * routes // (2 * experts))
    slot_total = experts * capacity
    chunked = experts & (experts - 1) == 0 and experts <= 8 and capacity % 16 == 0
    n_chunks = experts if chunked else 1
    units = gate_proj.shape[1] * n_dp
    flops = 2 * slot_total * width * units

    def shape(rows, cols, dtype=BF16):
        return jax.ShapeDtypeStruct((rows, cols), dtype)

    chunk_shapes = [shape(slot_total // n_chunks, width)] * n_chunks
    part_shapes = [shape(units // n_dp, width)] * n_dp

    gate_w = gather_shards(gate_proj[0], n_dp)
    up_w = gather_shards(up_proj[0], n_dp)
    down_w = gather_shards(down_proj[0], n_dp)

    me = (lax.axis_index("expert") if chunked else jnp.int32(0)).astype(jnp.int32).reshape(1)
    slots, *token_chunks = call(
        functools.partial(send_tokens_kernel, experts, capacity),
        [me, expert_ids.T, tokens],
        [shape(routes, tok_count, jnp.int32)] + chunk_shapes,
        flops // 10,
    )
    token_chunks = exchange(token_chunks, experts)
    cot_chunks = call(
        functools.partial(send_cots_kernel, experts, capacity),
        [slots, gate_scores.T, out_grad],
        chunk_shapes,
        flops // 10,
    )
    cot_chunks = exchange(cot_chunks, experts)

    received, hidden, act, slope = call(
        expert_in_kernel,
        [gate_w, up_w, *token_chunks],
        [shape(slot_total, width), shape(slot_total, units), shape(slot_total, units, F32), shape(slot_total, units, F32)],
        2 * flops,
    )
    out_chunks = call(expert_out_kernel, [hidden, down_w], chunk_shapes, flops)
    out_back = exchange(out_chunks, experts)

    cot_rows = call(join_kernel, cot_chunks, shape(slot_total, width))
    down_parts = call(weight_grad_kernel, [hidden, cot_rows], part_shapes, flops)
    gate_grad, up_grad = call(hidden_grad_kernel, [down_w, act, slope, cot_rows], [shape(slot_total, units)] * 2, flops)
    gate_parts = call(weight_grad_kernel, [gate_grad, received], part_shapes, flops)
    up_parts = call(weight_grad_kernel, [up_grad, received], part_shapes, flops)
    grad_chunks = call(input_grad_kernel, [gate_grad, up_grad, gate_w, up_w], chunk_shapes, 2 * flops)
    grad_back = exchange(grad_chunks, experts)

    down_out = scatter_sum(down_parts, n_dp)[None]
    gate_out = scatter_sum(gate_parts, n_dp)[None]
    up_out = scatter_sum(up_parts, n_dp)[None]

    output, d_scores = call(
        functools.partial(combine_out_kernel, slot_total),
        [slots, gate_scores, out_grad, *out_back],
        [shape(tok_count, width), shape(tok_count, routes, F32)],
        flops // 5,
    )
    d_tokens = call(
        functools.partial(combine_grad_kernel, slot_total), [slots, *grad_back], shape(tok_count, width), flops // 10
    )
    return (output, d_tokens, d_scores, gate_out, up_out, down_out)


def solution(mesh):
    rows = P(("expert", "dp"), None)
    weights = P("expert", "dp", None)
    return jax.shard_map(
        body,
        mesh=mesh,
        in_specs=(rows, rows, rows, weights, weights, weights, rows),
        out_specs=(rows, rows, rows, weights, weights, weights),
        check_vma=False,
    )
```

time: 247 us -> 245 us (level)
  starting transfers between devices: 20 us -> 64.2 us
  matrix products: 38 us -> 0 us
  Pallas kernels: 0 us -> 29.4 us
  other arithmetic: 14.7 us -> 0 us
  between operations: 14.3 us -> 0.88 us
  waiting for transfers between devices: 133 us -> 123 us
    all_to_all x4 -> x0, waiting for transfers between devices: 125 us -> none  [the longest x1 32 us: shards(): lax.all_to_all(outgoing.reshape(experts, capacity, model_width), 'expert'...]
    ppermute x0 -> x46, waiting for transfers between devices: none -> 123 us  [swap(): return lax.ppermute(value, axis, [(i, i ^ bits) for i in range(size)])]
    ppermute x0 -> x46, starting transfers between devices: none -> 64.2 us  [swap(): return lax.ppermute(value, axis, [(i, i ^ bits) for i in range(size)])]
    dot_general x9 -> x0, matrix products: 38 us -> none  [the longest x1 5.72 us: shards(): gate_pre = jnp.dot(received, gate_w.T, preferred_element_type=jnp.float32)]
    pallas_call x0 -> x21, Pallas kernels: none -> 29.4 us  [call(): pl.pallas_call(kernel, out_shape=shapes, in_specs=[SMEM if a.ndim == 1 el...]
    unnamed x29 -> x78, local copies, waits for them, and re-layouts: 3.71 us -> 27.4 us
    all_to_all x4 -> x0, starting transfers between devices: 19.6 us -> none  [the longest x1 7.41 us: shards(): lax.all_to_all(cot_slots.reshape(experts, capacity, model_width), 'expert...]
    reduce_sum x4 -> x0, other arithmetic: 10.5 us -> none  [the longest x1 5.59 us: shards(): jnp.sum((scores * pair_out).reshape(tok_count, routes_per, model_width),...]
  transfers between devices with their start and end apart: 10 -> 46, of which waited for: 5 -> 18; matrix products, arithmetic and copies ran while one was open for 27% -> 1% of each run, Pallas kernels for 0% -> 9%
where the time goes in v1:
time: 245 us; the launch traced here: 244 us
  waiting for transfers between devices  123 us (50%)
  starting transfers between devices  64.2 us (26%)
  Pallas kernels  29.4 us (12%)
  local copies, waits for them, and re-layouts  27.4 us (11%)
    ppermute x46, waiting for transfers between devices, swap(): return lax.ppermute(value, axis, [(i, i ^ bits) for i in range(size)])  123 us
    ppermute x46, starting transfers between devices, swap(): return lax.ppermute(value, axis, [(i, i ^ bits) for i in range(size)])  64.2 us
    pallas_call x21, Pallas kernels, call(): pl.pallas_call(kernel, out_shape=shapes, in_specs=[SMEM if a.ndim == 1 el...  29.4 us
    unnamed x78, local copies, waits for them, and re-layouts  27.4 us
  transfers between devices with their start and end apart: 46, of which 18 were waited for; matrix products, arithmetic and copies ran while one was open for 1% of the time, Pallas kernels for 9%

profile of v1, /device:TPU:0, one launch (start us, length us, event | category | flops | bytes accessed | tf_op | source)
XLA Modules:
  0.0 244.4 jit_solution(900439100700251846)
XLA Ops:
  0.6 1.0 copy-done.7
  3.0 3.0 %collective-permute-start.6 = (bf16[48,2048]{1,0:T(8,128)(2,1)S(1)}, bf16[48,2048]{1,0:T(8,128)(2,1)S(1)}, u32[]{:S(2)}, u32[]{:S(2)}) collective-permute-start(bf16[48,2048]{1,0:T(8,128)(2,1)S(1)} %get-tuple-element.61), channel_id=1, source_target_pairs={{0,4},{4,0},{8,12},{12,8},{16,20},{20,16},{24,28},{28,24},{1,5},{5... | collective-permute-start | bytes 589832 | tf_op jit(solution)/shard_map/ppermute | solution.py:206
  6.1 1.6 collective-permute-start.7
  7.7 1.0 copy-done
  10.6 3.0 %collective-permute-start.25 = (bf16[48,2048]{1,0:T(8,128)(2,1)S(1)}, bf16[48,2048]{1,0:T(8,128)(2,1)S(1)}, u32[]{:S(2)}, u32[]{:S(2)}) collective-permute-start(bf16[48,2048]{1,0:T(8,128)(2,1)S(1)} %get-tuple-element.83), channel_id=1, source_target_pairs={{0,12},{4,8},{8,4},{12,0},{16,28},{20,24},{24,20},{28,16},{1,13},{... | collective-permute-start | bytes 589832 | tf_op jit(solution)/shard_map/ppermute | solution.py:206
  13.5 2.6 %collective-permute-start.26 = (bf16[48,2048]{1,0:T(8,128)(2,1)S(1)}, bf16[48,2048]{1,0:T(8,128)(2,1)S(1)}, u32[]{:S(2)}, u32[]{:S(2)}) collective-permute-start(bf16[48,2048]{1,0:T(8,128)(2,1)S(1)} %get-tuple-element.84), channel_id=1, source_target_pairs={{0,16},{4,20},{8,24},{12,28},{16,0},{20,4},{24,8},{28,12},{1,17},{... | collective-permute-start | bytes 589832 | tf_op jit(solution)/shard_map/ppermute | solution.py:206
  16.1 1.5 collective-permute-start.1
  17.6 4.9 %collective-permute-done.24.refs_2_ = bf16[48,2048]{1,0:T(8,128)(2,1)S(1)} collective-permute-done((bf16[48,2048]{1,0:T(8,128)(2,1)S(1)}, bf16[48,2048]{1,0:T(8,128)(2,1)S(1)}, u32[]{:S(2)}, u32[]{:S(2)}) %collective-permute-start.24) | collective-permute-done | bytes 196640 | tf_op jit(solution)/shard_map/ppermute | solution.py:206
  22.5 1.5 collective-permute-start.4
  24.1 1.6 collective-permute-done.25.refs_3_
  25.7 1.5 collective-permute-start.14
  27.2 1.0 collective-permute-start.27
  28.3 9.6 %collective-permute-done.27.refs_5_ = bf16[48,2048]{1,0:T(8,128)(2,1)S(1)} collective-permute-done((bf16[48,2048]{1,0:T(8,128)(2,1)S(1)}, bf16[48,2048]{1,0:T(8,128)(2,1)S(1)}, u32[]{:S(2)}, u32[]{:S(2)}) %collective-permute-start.27) | collective-permute-done | bytes 196640 | tf_op jit(solution)/shard_map/ppermute | solution.py:206
  37.9 2.5 %collective-permute-start.28 = (bf16[48,2048]{1,0:T(8,128)(2,1)S(1)}, bf16[48,2048]{1,0:T(8,128)(2,1)S(1)}, u32[]{:S(2)}, u32[]{:S(2)}) collective-permute-start(bf16[48,2048]{1,0:T(8,128)(2,1)S(1)} %get-tuple-element.86), channel_id=1, source_target_pairs={{0,24},{4,28},{8,16},{12,20},{16,8},{20,12},{24,0},{28,4},{1,25},{... | collective-permute-start | bytes 589832 | tf_op jit(solution)/shard_map/ppermute | solution.py:206
  40.4 5.3 %collective-permute-done.28.refs_6_ = bf16[48,2048]{1,0:T(8,128)(2,1)S(1)} collective-permute-done((bf16[48,2048]{1,0:T(8,128)(2,1)S(1)}, bf16[48,2048]{1,0:T(8,128)(2,1)S(1)}, u32[]{:S(2)}, u32[]{:S(2)}) %collective-permute-start.28) | collective-permute-done | bytes 196640 | tf_op jit(solution)/shard_map/ppermute | solution.py:206
  45.7 2.8 %collective-permute-start.29 = (bf16[48,2048]{1,0:T(8,128)(2,1)S(1)}, bf16[48,2048]{1,0:T(8,128)(2,1)S(1)}, u32[]{:S(2)}, u32[]{:S(2)}) collective-permute-start(bf16[48,2048]{1,0:T(8,128)(2,1)S(1)} %get-tuple-element.87), channel_id=1, source_target_pairs={{0,28},{4,24},{8,20},{12,16},{16,12},{20,8},{24,4},{28,0},{1,29},{... | collective-permute-start | bytes 589832 | tf_op jit(solution)/shard_map/ppermute | solution.py:206
  48.5 5.7 %collective-permute-done.29.refs_7_ = bf16[48,2048]{1,0:T(8,128)(2,1)S(1)} collective-permute-done((bf16[48,2048]{1,0:T(8,128)(2,1)S(1)}, bf16[48,2048]{1,0:T(8,128)(2,1)S(1)}, u32[]{:S(2)}, u32[]{:S(2)}) %collective-permute-start.29) | collective-permute-done | bytes 196640 | tf_op jit(solution)/shard_map/ppermute | solution.py:206
  55.2 12.4 %collective-permute-done.14.refs_2_ = bf16[192,2048]{1,0:T(8,128)(2,1)S(1)} collective-permute-done((bf16[192,2048]{1,0:T(8,128)(2,1)}, bf16[192,2048]{1,0:T(8,128)(2,1)S(1)}, u32[]{:S(2)}, u32[]{:S(2)}) %collective-permute-start.14) | collective-permute-done | bytes 786464 | tf_op jit(solution)/shard_map/ppermute | solution.py:206
  68.7 3.2 %collective-permute-start.10 = (bf16[48,2048]{1,0:T(8,128)(2,1)S(1)}, bf16[48,2048]{1,0:T(8,128)(2,1)S(1)}, u32[]{:S(2)}, u32[]{:S(2)}) collective-permute-start(bf16[48,2048]{1,0:T(8,128)(2,1)S(1)} %get-tuple-element.65), channel_id=1, source_target_pairs={{0,20},{4,16},{8,28},{12,24},{16,4},{20,0},{24,12},{28,8},{1,21},{... | collective-permute-start | bytes 589832 | tf_op jit(solution)/shard_map/ppermute | solution.py:206
  71.9 1.4 collective-permute-start.11
  73.3 2.8 %collective-permute-start.12 = (bf16[48,2048]{1,0:T(8,128)(2,1)S(1)}, bf16[48,2048]{1,0:T(8,128)(2,1)S(1)}, u32[]{:S(2)}, u32[]{:S(2)}) collective-permute-start(bf16[48,2048]{1,0:T(8,128)(2,1)S(1)} %get-tuple-element.67), channel_id=1, source_target_pairs={{0,28},{4,24},{8,20},{12,16},{16,12},{20,8},{24,4},{28,0},{1,29},{... | collective-permute-start | bytes 589832 | tf_op jit(solution)/shard_map/ppermute | solution.py:206
  76.2 1.0 copy-done.2
  77.4 0.9 copy-done.3
  79.7 14.3 %collective-permute-done.9.refs_4_ = bf16[48,2048]{1,0:T(8,128)(2,1)S(1)} collective-permute-done((bf16[48,2048]{1,0:T(8,128)(2,1)S(1)}, bf16[48,2048]{1,0:T(8,128)(2,1)S(1)}, u32[]{:S(2)}, u32[]{:S(2)}) %collective-permute-start.9) | collective-permute-done | bytes 196640 | tf_op jit(solution)/shard_map/ppermute | solution.py:206
  94.0 4.8 %collective-permute-done.10.refs_5_ = bf16[48,2048]{1,0:T(8,128)(2,1)S(1)} collective-permute-done((bf16[48,2048]{1,0:T(8,128)(2,1)S(1)}, bf16[48,2048]{1,0:T(8,128)(2,1)S(1)}, u32[]{:S(2)}, u32[]{:S(2)}) %collective-permute-start.10) | collective-permute-done | bytes 196640 | tf_op jit(solution)/shard_map/ppermute | solution.py:206
  98.8 2.7 %shard_map.121 = (bf16[384,2048]{1,0:T(8,128)(2,1)S(1)}, bf16[384,768]{1,0:T(8,128)(2,1)S(1)}, f32[384,768]{1,0:T(8,128)S(1)}, f32[384,768]{1,0:T(8,128)S(1)}) custom-call(bf16[768,2048]{1,0:T(8,128)(2,1)S(1)} %shard_map.119.gate_ref, bf16[768,2048]{1,0:T(8,128)(2,1)S(1)} %shard_map.120.up_ref, bf16[48,2048]{1,0:T(8,128)(2,1)S(1)} %get-tuple-element.60.refs_0_, ...), custom_call_target="tpu_custom_call" | custom-call | flops 2415919104 | tf_op jit(solution)/shard_map/pallas_call | solution.py:195
  101.5 1.4 shard_map.123
  102.9 1.0 collective-permute-start.16
  103.8 8.2 %collective-permute-start.17 = (bf16[48,2048]{1,0:T(8,128)(2,1)S(1)}, bf16[48,2048]{1,0:T(8,128)(2,1)S(1)}, u32[]{:S(2)}, u32[]{:S(2)}) collective-permute-start(bf16[48,2048]{1,0:T(8,128)(2,1)S(1)} %get-tuple-element.71), channel_id=1, source_target_pairs={{0,8},{4,12},{8,0},{12,4},{16,24},{20,28},{24,16},{28,20},{1,9},{5... | collective-permute-start | bytes 589832 | tf_op jit(solution)/shard_map/ppermute | solution.py:206
  112.7 1.9 collective-permute-start.19
  114.6 1.3 collective-permute-start.20
  115.9 1.8 shard_map.136
  117.7 1.4 shard_map.127
  119.2 1.9 shard_map.133
  121.0 2.0 shard_map.130
  123.0 1.5 collective-permute-start.21
  124.6 3.1 %collective-permute-start.22 = (bf16[48,2048]{1,0:T(8,128)(2,1)S(1)}, bf16[48,2048]{1,0:T(8,128)(2,1)S(1)}, u32[]{:S(2)}, u32[]{:S(2)}) collective-permute-start(bf16[48,2048]{1,0:T(8,128)(2,1)S(1)} %get-tuple-element.76), channel_id=1, source_target_pairs={{0,28},{4,24},{8,20},{12,16},{16,12},{20,8},{24,4},{28,0},{1,29},{... | collective-permute-start | bytes 589832 | tf_op jit(solution)/shard_map/ppermute | solution.py:206
  128.6 9.6 %collective-permute-done.19.refs_4_ = bf16[48,2048]{1,0:T(8,128)(2,1)S(1)} collective-permute-done((bf16[48,2048]{1,0:T(8,128)(2,1)S(1)}, bf16[48,2048]{1,0:T(8,128)(2,1)S(1)}, u32[]{:S(2)}, u32[]{:S(2)}) %collective-permute-start.19) | collective-permute-done | bytes 196640 | tf_op jit(solution)/shard_map/ppermute | solution.py:206
  138.9 3.3 %collective-permute-done.20.refs_5_ = bf16[48,2048]{1,0:T(8,128)(2,1)S(1)} collective-permute-done((bf16[48,2048]{1,0:T(8,128)(2,1)S(1)}, bf16[48,2048]{1,0:T(8,128)(2,1)S(1)}, u32[]{:S(2)}, u32[]{:S(2)}) %collective-permute-start.20) | collective-permute-done | bytes 196640 | tf_op jit(solution)/shard_map/ppermute | solution.py:206
  142.9 2.6 %shard_map.128 = (bf16[48,2048]{1,0:T(8,128)(2,1)S(1)}, bf16[48,2048]{1,0:T(8,128)(2,1)S(1)}, bf16[48,2048]{1,0:T(8,128)(2,1)S(1)}, bf16[48,2048]{1,0:T(8,128)(2...) custom-call(bf16[384,768]{1,0:T(8,128)(2,1)S(1)} %get-tuple-element., ...), custom_call_target="tpu_custom_call" | custom-call | flops 2415919104 | tf_op jit(solution)/shard_map/pallas_call | solution.py:195
  145.5 1.8 collective-permute-start.30
  147.5 5.4 %collective-permute-done.30.refs_1_ = bf16[48,2048]{1,0:T(8,128)(2,1)S(1)} collective-permute-done((bf16[48,2048]{1,0:T(8,128)(2,1)S(1)}, bf16[48,2048]{1,0:T(8,128)(2,1)S(1)}, u32[]{:S(2)}, u32[]{:S(2)}) %collective-permute-start.30) | collective-permute-done | bytes 196640 | tf_op jit(solution)/shard_map/ppermute | solution.py:206
  153.5 5.8 %collective-permute-done.31.refs_2_ = bf16[48,2048]{1,0:T(8,128)(2,1)S(1)} collective-permute-done((bf16[48,2048]{1,0:T(8,128)(2,1)S(1)}, bf16[48,2048]{1,0:T(8,128)(2,1)S(1)}, u32[]{:S(2)}, u32[]{:S(2)}) %collective-permute-start.31) | collective-permute-done | bytes 196640 | tf_op jit(solution)/shard_map/ppermute | solution.py:206
  159.3 1.4 collective-permute-start.32
  160.8 5.1 %collective-permute-done.32.refs_3_ = bf16[48,2048]{1,0:T(8,128)(2,1)S(1)} collective-permute-done((bf16[48,2048]{1,0:T(8,128)(2,1)S(1)}, bf16[48,2048]{1,0:T(8,128)(2,1)S(1)}, u32[]{:S(2)}, u32[]{:S(2)}) %collective-permute-start.32) | collective-permute-done | bytes 196640 | tf_op jit(solution)/shard_map/ppermute | solution.py:206
  165.9 1.6 collective-permute-start.33
  167.5 2.5 %collective-permute-start.34 = (bf16[48,2048]{1,0:T(8,128)(2,1)S(1)}, bf16[48,2048]{1,0:T(8,128)(2,1)S(1)}, u32[]{:S(2)}, u32[]{:S(2)}) collective-permute-start(bf16[48,2048]{1,0:T(8,128)(2,1)S(1)} %get-tuple-element.95), channel_id=1, source_target_pairs={{0,20},{4,16},{8,28},{12,24},{16,4},{20,0},{24,12},{28,8},{1,21},{... | collective-permute-start | bytes 589832 | tf_op jit(solution)/shard_map/ppermute | solution.py:206
  170.7 2.8 %collective-permute-start.36 = (bf16[48,2048]{1,0:T(8,128)(2,1)S(1)}, bf16[48,2048]{1,0:T(8,128)(2,1)S(1)}, u32[]{:S(2)}, u32[]{:S(2)}) collective-permute-start(bf16[48,2048]{1,0:T(8,128)(2,1)S(1)} %get-tuple-element.97), channel_id=1, source_target_pairs={{0,28},{4,24},{8,20},{12,16},{16,12},{20,8},{24,4},{28,0},{1,29},{... | collective-permute-start | bytes 589832 | tf_op jit(solution)/shard_map/ppermute | solution.py:206
  173.6 1.1 shard_map.137
  174.6 1.1 shard_map.134
  175.8 1.1 shard_map.131
  176.8 11.8 %collective-permute-done.33.refs_4_ = bf16[48,2048]{1,0:T(8,128)(2,1)S(1)} collective-permute-done((bf16[48,2048]{1,0:T(8,128)(2,1)S(1)}, bf16[48,2048]{1,0:T(8,128)(2,1)S(1)}, u32[]{:S(2)}, u32[]{:S(2)}) %collective-permute-start.33) | collective-permute-done | bytes 196640 | tf_op jit(solution)/shard_map/ppermute | solution.py:206
  189.3 1.5 collective-permute-start.45
  190.8 3.2 %collective-permute-done.34.refs_5_ = bf16[48,2048]{1,0:T(8,128)(2,1)S(1)} collective-permute-done((bf16[48,2048]{1,0:T(8,128)(2,1)S(1)}, bf16[48,2048]{1,0:T(8,128)(2,1)S(1)}, u32[]{:S(2)}, u32[]{:S(2)}) %collective-permute-start.34) | collective-permute-done | bytes 196640 | tf_op jit(solution)/shard_map/ppermute | solution.py:206
  195.4 1.5 collective-permute-start.42
  204.0 1.8 shard_map.124
  206.4 1.5 copy.14
  215.3 1.3 shard_map.129
  216.6 1.1 copy-done.6
  217.7 2.3 shard_map.138
  220.0 6.9 %collective-permute-done.42.refs_2_ = bf16[192,2048]{1,0:T(8,128)(2,1)} collective-permute-done((bf16[192,2048]{1,0:T(8,128)(2,1)}, bf16[192,2048]{1,0:T(8,128)(2,1)}, u32[]{:S(2)}, u32[]{:S(2)}) %collective-permute-start.42) | collective-permute-done | bytes 786464 | tf_op jit(solution)/shard_map/ppermute | solution.py:206
  226.9 2.5 %shard_map.135 = bf16[192,2048]{1,0:T(8,128)(2,1)} custom-call(bf16[192,2048]{1,0:T(8,128)(2,1)S(1)} %get-tuple-element.104.refs_0_, bf16[192,2048]{1,0:T(8,128)(2,1)} %collective-permute-done.40.refs_1_, bf16[192,2048]{1,0:T(8,128)(2,1)} %collective-permute-done.42.refs_2_), custom_call_target="tpu_custom_call" | custom-call | tf_op jit(solution)/shard_map/pallas_call | solution.py:195
  229.4 12.4 %collective-permute-done.39.refs_2_ = bf16[192,2048]{1,0:T(8,128)(2,1)} collective-permute-done((bf16[192,2048]{1,0:T(8,128)(2,1)}, bf16[192,2048]{1,0:T(8,128)(2,1)}, u32[]{:S(2)}, u32[]{:S(2)}) %collective-permute-start.39) | collective-permute-done | bytes 786464 | tf_op jit(solution)/shard_map/ppermute | solution.py:206
  241.8 2.5 %shard_map.132 = bf16[192,2048]{1,0:T(8,128)(2,1)} custom-call(bf16[192,2048]{1,0:T(8,128)(2,1)S(1)} %get-tuple-element.100.refs_0_, bf16[192,2048]{1,0:T(8,128)(2,1)} %collective-permute-done.37.refs_1_, bf16[192,2048]{1,0:T(8,128)(2,1)} %collective-permute-done.39.refs_2_), custom_call_target="tpu_custom_call" | custom-call | tf_op jit(solution)/shard_map/pallas_call | solution.py:195
  (127 shorter events, 28.7 us)
Async XLA Ops:
  0.6 1.0 copy-start.7
  3.0 10.5 %collective-permute-start.6 = (bf16[48,2048]{1,0:T(8,128)(2,1)S(1)}, bf16[48,2048]{1,0:T(8,128)(2,1)S(1)}, u32[]{:S(2)}, u32[]{:S(2)}) collective-permute-start(bf16[48,2048]{1,0:T(8,128)(2,1)S(1)} %get-tuple-element.61), channel_id=1, source_target_pairs={{0,4},{4,0},{8,12},{12,8},{16,20},{20,16},{24,28},{28,24},{1,5},{5... | collective-permute-start | bytes 589832 | tf_op jit(solution)/shard_map/ppermute | solution.py:206
  6.1 10.0 %collective-permute-start.7 = (bf16[48,2048]{1,0:T(8,128)(2,1)S(1)}, bf16[48,2048]{1,0:T(8,128)(2,1)S(1)}, u32[]{:S(2)}, u32[]{:S(2)}) collective-permute-start(bf16[48,2048]{1,0:T(8,128)(2,1)S(1)} %get-tuple-element.62), channel_id=1, source_target_pairs={{0,8},{4,12},{8,0},{12,4},{16,24},{20,28},{24,16},{28,20},{1,9},{5... | collective-permute-start | bytes 589832 | tf_op jit(solution)/shard_map/ppermute | solution.py:206
  7.7 1.0 copy-start
  10.0 7.7 %collective-permute-start.23 = (bf16[48,2048]{1,0:T(8,128)(2,1)S(1)}, bf16[48,2048]{1,0:T(8,128)(2,1)S(1)}, u32[]{:S(2)}, u32[]{:S(2)}) collective-permute-start(bf16[48,2048]{1,0:T(8,128)(2,1)S(1)} %get-tuple-element.81), channel_id=1, source_target_pairs={{0,4},{4,0},{8,12},{12,8},{16,20},{20,16},{24,28},{28,24},{1,5},{5... | collective-permute-start | bytes 589832 | tf_op jit(solution)/shard_map/ppermute | solution.py:206
  10.6 12.0 %collective-permute-start.24 = (bf16[48,2048]{1,0:T(8,128)(2,1)S(1)}, bf16[48,2048]{1,0:T(8,128)(2,1)S(1)}, u32[]{:S(2)}, u32[]{:S(2)}) collective-permute-start(bf16[48,2048]{1,0:T(8,128)(2,1)S(1)} %get-tuple-element.82), channel_id=1, source_target_pairs={{0,8},{4,12},{8,0},{12,4},{16,24},{20,28},{24,16},{28,20},{1,9},{5... | collective-permute-start | bytes 589832 | tf_op jit(solution)/shard_map/ppermute | solution.py:206
  10.6 15.2 %collective-permute-start.25 = (bf16[48,2048]{1,0:T(8,128)(2,1)S(1)}, bf16[48,2048]{1,0:T(8,128)(2,1)S(1)}, u32[]{:S(2)}, u32[]{:S(2)}) collective-permute-start(bf16[48,2048]{1,0:T(8,128)(2,1)S(1)} %get-tuple-element.83), channel_id=1, source_target_pairs={{0,12},{4,8},{8,4},{12,0},{16,28},{20,24},{24,20},{28,16},{1,13},{... | collective-permute-start | bytes 589832 | tf_op jit(solution)/shard_map/ppermute | solution.py:206
  13.5 13.7 %collective-permute-start.26 = (bf16[48,2048]{1,0:T(8,128)(2,1)S(1)}, bf16[48,2048]{1,0:T(8,128)(2,1)S(1)}, u32[]{:S(2)}, u32[]{:S(2)}) collective-permute-start(bf16[48,2048]{1,0:T(8,128)(2,1)S(1)} %get-tuple-element.84), channel_id=1, source_target_pairs={{0,16},{4,20},{8,24},{12,28},{16,0},{20,4},{24,8},{28,12},{1,17},{... | collective-permute-start | bytes 589832 | tf_op jit(solution)/shard_map/ppermute | solution.py:206
  16.1 38.1 %collective-permute-start.1 = (bf16[192,2048]{1,0:T(8,128)(2,1)}, bf16[192,2048]{1,0:T(8,128)(2,1)S(1)}, u32[]{:S(2)}, u32[]{:S(2)}) collective-permute-start(bf16[192,2048]{1,0:T(8,128)(2,1)} %bitcast.9), channel_id=1, source_target_pairs={{0,2},{1,3},{2,0},{3,1},{4,6},{5,7},{6,4},{7,5},{8,10},{9,11},{10,... | collective-permute-start | bytes 2359304 | tf_op jit(solution)/shard_map/ppermute | solution.py:206
  17.6 37.1 %collective-permute-start = (bf16[192,2048]{1,0:T(8,128)(2,1)}, bf16[192,2048]{1,0:T(8,128)(2,1)S(1)}, u32[]{:S(2)}, u32[]{:S(2)}) collective-permute-start(bf16[192,2048]{1,0:T(8,128)(2,1)} %bitcast.10), channel_id=1, source_target_pairs={{0,1},{1,0},{2,3},{3,2},{4,5},{5,4},{6,7},{7,6},{8,9},{9,8},{10,11... | collective-permute-start | bytes 2359304 | tf_op jit(solution)/shard_map/ppermute | solution.py:206
  22.5 32.2 %collective-permute-start.4 = (bf16[192,2048]{1,0:T(8,128)(2,1)}, bf16[192,2048]{1,0:T(8,128)(2,1)S(1)}, u32[]{:S(2)}, u32[]{:S(2)}) collective-permute-start(bf16[192,2048]{1,0:T(8,128)(2,1)} %bitcast.12), channel_id=1, source_target_pairs={{0,2},{1,3},{2,0},{3,1},{4,6},{5,7},{6,4},{7,5},{8,10},{9,11},{10,... | collective-permute-start | bytes 2359304 | tf_op jit(solution)/shard_map/ppermute | solution.py:206
  25.7 41.9 %collective-permute-start.14 = (bf16[192,2048]{1,0:T(8,128)(2,1)}, bf16[192,2048]{1,0:T(8,128)(2,1)S(1)}, u32[]{:S(2)}, u32[]{:S(2)}) collective-permute-start(bf16[192,2048]{1,0:T(8,128)(2,1)} %bitcast.15), channel_id=1, source_target_pairs={{0,2},{1,3},{2,0},{3,1},{4,6},{5,7},{6,4},{7,5},{8,10},{9,11},{10,... | collective-permute-start | bytes 2359304 | tf_op jit(solution)/shard_map/ppermute | solution.py:206
  27.2 10.7 %collective-permute-start.27 = (bf16[48,2048]{1,0:T(8,128)(2,1)S(1)}, bf16[48,2048]{1,0:T(8,128)(2,1)S(1)}, u32[]{:S(2)}, u32[]{:S(2)}) collective-permute-start(bf16[48,2048]{1,0:T(8,128)(2,1)S(1)} %get-tuple-element.85), channel_id=1, source_target_pairs={{0,20},{4,16},{8,28},{12,24},{16,4},{20,0},{24,12},{28,8},{1,21},{... | collective-permute-start | bytes 589832 | tf_op jit(solution)/shard_map/ppermute | solution.py:206
  37.9 7.8 %collective-permute-start.28 = (bf16[48,2048]{1,0:T(8,128)(2,1)S(1)}, bf16[48,2048]{1,0:T(8,128)(2,1)S(1)}, u32[]{:S(2)}, u32[]{:S(2)}) collective-permute-start(bf16[48,2048]{1,0:T(8,128)(2,1)S(1)} %get-tuple-element.86), channel_id=1, source_target_pairs={{0,24},{4,28},{8,16},{12,20},{16,8},{20,12},{24,0},{28,4},{1,25},{... | collective-permute-start | bytes 589832 | tf_op jit(solution)/shard_map/ppermute | solution.py:206
  45.7 8.5 %collective-permute-start.29 = (bf16[48,2048]{1,0:T(8,128)(2,1)S(1)}, bf16[48,2048]{1,0:T(8,128)(2,1)S(1)}, u32[]{:S(2)}, u32[]{:S(2)}) collective-permute-start(bf16[48,2048]{1,0:T(8,128)(2,1)S(1)} %get-tuple-element.87), channel_id=1, source_target_pairs={{0,28},{4,24},{8,20},{12,16},{16,12},{20,8},{24,4},{28,0},{1,29},{... | collective-permute-start | bytes 589832 | tf_op jit(solution)/shard_map/ppermute | solution.py:206
  54.2 13.4 %collective-permute-start.3 = (bf16[192,2048]{1,0:T(8,128)(2,1)}, bf16[192,2048]{1,0:T(8,128)(2,1)S(1)}, u32[]{:S(2)}, u32[]{:S(2)}) collective-permute-start(bf16[192,2048]{1,0:T(8,128)(2,1)} %bitcast.13), channel_id=1, source_target_pairs={{0,1},{1,0},{2,3},{3,2},{4,5},{5,4},{6,7},{7,6},{8,9},{9,8},{10,11... | collective-permute-start | bytes 2359304 | tf_op jit(solution)/shard_map/ppermute | solution.py:206
  54.2 14.2 %collective-permute-start.13 = (bf16[192,2048]{1,0:T(8,128)(2,1)}, bf16[192,2048]{1,0:T(8,128)(2,1)S(1)}, u32[]{:S(2)}, u32[]{:S(2)}) collective-permute-start(bf16[192,2048]{1,0:T(8,128)(2,1)} %bitcast.16), channel_id=1, source_target_pairs={{0,1},{1,0},{2,3},{3,2},{4,5},{5,4},{6,7},{7,6},{8,9},{9,8},{10,11... | collective-permute-start | bytes 2359304 | tf_op jit(solution)/shard_map/ppermute | solution.py:206
  54.7 14.0 %collective-permute-start.2 = (bf16[192,2048]{1,0:T(8,128)(2,1)S(1)}, bf16[192,2048]{1,0:T(8,128)(2,1)S(1)}, u32[]{:S(2)}, u32[]{:S(2)}) collective-permute-start(bf16[192,2048]{1,0:T(8,128)(2,1)S(1)} %collective-permute-done.1.refs_2_), channel_id=1, source_target_pairs={{0,1},{1,0},{2,3},{3,2},{4,5},{5,4},{6,7},{7,6},{8,9},{9,8},{10,11... | collective-permute-start | bytes 2359304 | tf_op jit(solution)/shard_map/ppermute | solution.py:206
  54.8 17.1 %collective-permute-start.5 = (bf16[192,2048]{1,0:T(8,128)(2,1)S(1)}, bf16[192,2048]{1,0:T(8,128)(2,1)S(1)}, u32[]{:S(2)}, u32[]{:S(2)}) collective-permute-start(bf16[192,2048]{1,0:T(8,128)(2,1)S(1)} %collective-permute-done.4.refs_2_), channel_id=1, source_target_pairs={{0,1},{1,0},{2,3},{3,2},{4,5},{5,4},{6,7},{7,6},{8,9},{9,8},{10,11... | collective-permute-start | bytes 2359304 | tf_op jit(solution)/shard_map/ppermute | solution.py:206
  67.6 5.7 %collective-permute-start.15 = (bf16[192,2048]{1,0:T(8,128)(2,1)S(1)}, bf16[192,2048]{1,0:T(8,128)(2,1)S(1)}, u32[]{:S(2)}, u32[]{:S(2)}) collective-permute-start(bf16[192,2048]{1,0:T(8,128)(2,1)S(1)} %collective-permute-done.14.refs_2_), channel_id=1, source_target_pairs={{0,1},{1,0},{2,3},{3,2},{4,5},{5,4},{6,7},{7,6},{8,9},{9,8},{10,11... | collective-permute-start | bytes 2359304 | tf_op jit(solution)/shard_map/ppermute | solution.py:206
  67.6 12.0 %collective-permute-start.8 = (bf16[48,2048]{1,0:T(8,128)(2,1)S(1)}, bf16[48,2048]{1,0:T(8,128)(2,1)S(1)}, u32[]{:S(2)}, u32[]{:S(2)}) collective-permute-start(bf16[48,2048]{1,0:T(8,128)(2,1)S(1)} %get-tuple-element.63), channel_id=1, source_target_pairs={{0,12},{4,8},{8,4},{12,0},{16,28},{20,24},{24,20},{28,16},{1,13},{... | collective-permute-start | bytes 589832 | tf_op jit(solution)/shard_map/ppermute | solution.py:206
  68.4 25.6 %collective-permute-start.9 = (bf16[48,2048]{1,0:T(8,128)(2,1)S(1)}, bf16[48,2048]{1,0:T(8,128)(2,1)S(1)}, u32[]{:S(2)}, u32[]{:S(2)}) collective-permute-start(bf16[48,2048]{1,0:T(8,128)(2,1)S(1)} %get-tuple-element.64), channel_id=1, source_target_pairs={{0,16},{4,20},{8,24},{12,28},{16,0},{20,4},{24,8},{28,12},{1,17},{... | collective-permute-start | bytes 589832 | tf_op jit(solution)/shard_map/ppermute | solution.py:206
  68.7 30.0 %collective-permute-start.10 = (bf16[48,2048]{1,0:T(8,128)(2,1)S(1)}, bf16[48,2048]{1,0:T(8,128)(2,1)S(1)}, u32[]{:S(2)}, u32[]{:S(2)}) collective-permute-start(bf16[48,2048]{1,0:T(8,128)(2,1)S(1)} %get-tuple-element.65), channel_id=1, source_target_pairs={{0,20},{4,16},{8,28},{12,24},{16,4},{20,0},{24,12},{28,8},{1,21},{... | collective-permute-start | bytes 589832 | tf_op jit(solution)/shard_map/ppermute | solution.py:206
  71.9 26.9 %collective-permute-start.11 = (bf16[48,2048]{1,0:T(8,128)(2,1)S(1)}, bf16[48,2048]{1,0:T(8,128)(2,1)S(1)}, u32[]{:S(2)}, u32[]{:S(2)}) collective-permute-start(bf16[48,2048]{1,0:T(8,128)(2,1)S(1)} %get-tuple-element.66), channel_id=1, source_target_pairs={{0,24},{4,28},{8,16},{12,20},{16,8},{20,12},{24,0},{28,4},{1,25},{... | collective-permute-start | bytes 589832 | tf_op jit(solution)/shard_map/ppermute | solution.py:206
  73.3 25.5 %collective-permute-start.12 = (bf16[48,2048]{1,0:T(8,128)(2,1)S(1)}, bf16[48,2048]{1,0:T(8,128)(2,1)S(1)}, u32[]{:S(2)}, u32[]{:S(2)}) collective-permute-start(bf16[48,2048]{1,0:T(8,128)(2,1)S(1)} %get-tuple-element.67), channel_id=1, source_target_pairs={{0,28},{4,24},{8,20},{12,16},{16,12},{20,8},{24,4},{28,0},{1,29},{... | collective-permute-start | bytes 589832 | tf_op jit(solution)/shard_map/ppermute | solution.py:206
  76.1 1.1 copy-start.2
  77.2 1.1 copy-start.3
  78.3 1.1 copy-start.4
  102.9 20.1 %collective-permute-start.16 = (bf16[48,2048]{1,0:T(8,128)(2,1)S(1)}, bf16[48,2048]{1,0:T(8,128)(2,1)S(1)}, u32[]{:S(2)}, u32[]{:S(2)}) collective-permute-start(bf16[48,2048]{1,0:T(8,128)(2,1)S(1)} %get-tuple-element.70), channel_id=1, source_target_pairs={{0,4},{4,0},{8,12},{12,8},{16,20},{20,16},{24,28},{28,24},{1,5},{5... | collective-permute-start | bytes 589832 | tf_op jit(solution)/shard_map/ppermute | solution.py:206
  103.8 20.7 %collective-permute-start.17 = (bf16[48,2048]{1,0:T(8,128)(2,1)S(1)}, bf16[48,2048]{1,0:T(8,128)(2,1)S(1)}, u32[]{:S(2)}, u32[]{:S(2)}) collective-permute-start(bf16[48,2048]{1,0:T(8,128)(2,1)S(1)} %get-tuple-element.71), channel_id=1, source_target_pairs={{0,8},{4,12},{8,0},{12,4},{16,24},{20,28},{24,16},{28,20},{1,9},{5... | collective-permute-start | bytes 589832 | tf_op jit(solution)/shard_map/ppermute | solution.py:206
  112.1 15.8 %collective-permute-start.18 = (bf16[48,2048]{1,0:T(8,128)(2,1)S(1)}, bf16[48,2048]{1,0:T(8,128)(2,1)S(1)}, u32[]{:S(2)}, u32[]{:S(2)}) collective-permute-start(bf16[48,2048]{1,0:T(8,128)(2,1)S(1)} %get-tuple-element.72), channel_id=1, source_target_pairs={{0,12},{4,8},{8,4},{12,0},{16,28},{20,24},{24,20},{28,16},{1,13},{... | collective-permute-start | bytes 589832 | tf_op jit(solution)/shard_map/ppermute | solution.py:206
  112.7 25.5 %collective-permute-start.19 = (bf16[48,2048]{1,0:T(8,128)(2,1)S(1)}, bf16[48,2048]{1,0:T(8,128)(2,1)S(1)}, u32[]{:S(2)}, u32[]{:S(2)}) collective-permute-start(bf16[48,2048]{1,0:T(8,128)(2,1)S(1)} %get-tuple-element.73), channel_id=1, source_target_pairs={{0,16},{4,20},{8,24},{12,28},{16,0},{20,4},{24,8},{28,12},{1,17},{... | collective-permute-start | bytes 589832 | tf_op jit(solution)/shard_map/ppermute | solution.py:206
  114.6 27.6 %collective-permute-start.20 = (bf16[48,2048]{1,0:T(8,128)(2,1)S(1)}, bf16[48,2048]{1,0:T(8,128)(2,1)S(1)}, u32[]{:S(2)}, u32[]{:S(2)}) collective-permute-start(bf16[48,2048]{1,0:T(8,128)(2,1)S(1)} %get-tuple-element.74), channel_id=1, source_target_pairs={{0,20},{4,16},{8,28},{12,24},{16,4},{20,0},{24,12},{28,8},{1,21},{... | collective-permute-start | bytes 589832 | tf_op jit(solution)/shard_map/ppermute | solution.py:206
  123.0 22.4 %collective-permute-start.21 = (bf16[48,2048]{1,0:T(8,128)(2,1)S(1)}, bf16[48,2048]{1,0:T(8,128)(2,1)S(1)}, u32[]{:S(2)}, u32[]{:S(2)}) collective-permute-start(bf16[48,2048]{1,0:T(8,128)(2,1)S(1)} %get-tuple-element.75), channel_id=1, source_target_pairs={{0,24},{4,28},{8,16},{12,20},{16,8},{20,12},{24,0},{28,4},{1,25},{... | collective-permute-start | bytes 589832 | tf_op jit(solution)/shard_map/ppermute | solution.py:206
  124.6 22.7 %collective-permute-start.22 = (bf16[48,2048]{1,0:T(8,128)(2,1)S(1)}, bf16[48,2048]{1,0:T(8,128)(2,1)S(1)}, u32[]{:S(2)}, u32[]{:S(2)}) collective-permute-start(bf16[48,2048]{1,0:T(8,128)(2,1)S(1)} %get-tuple-element.76), channel_id=1, source_target_pairs={{0,28},{4,24},{8,20},{12,16},{16,12},{20,8},{24,4},{28,0},{1,29},{... | collective-permute-start | bytes 589832 | tf_op jit(solution)/shard_map/ppermute | solution.py:206
  128.6 38.9 %collective-permute-start.44 = (bf16[192,2048]{1,0:T(8,128)(2,1)S(1)}, bf16[192,2048]{1,0:T(8,128)(2,1)S(1)}, u32[]{:S(2)}, u32[]{:S(2)}) collective-permute-start(bf16[192,2048]{1,0:T(8,128)(2,1)S(1)} %get-tuple-element.111), channel_id=1, source_target_pairs={{0,1},{1,0},{2,3},{3,2},{4,5},{5,4},{6,7},{7,6},{8,9},{9,8},{10,11... | collective-permute-start | bytes 2359304 | tf_op jit(solution)/shard_map/ppermute | solution.py:206
  138.9 31.1 %collective-permute-start.41 = (bf16[192,2048]{1,0:T(8,128)(2,1)S(1)}, bf16[192,2048]{1,0:T(8,128)(2,1)S(1)}, u32[]{:S(2)}, u32[]{:S(2)}) collective-permute-start(bf16[192,2048]{1,0:T(8,128)(2,1)S(1)} %get-tuple-element.107), channel_id=1, source_target_pairs={{0,1},{1,0},{2,3},{3,2},{4,5},{5,4},{6,7},{7,6},{8,9},{9,8},{10,11... | collective-permute-start | bytes 2359304 | tf_op jit(solution)/shard_map/ppermute | solution.py:206
  142.9 27.9 %collective-permute-start.38 = (bf16[192,2048]{1,0:T(8,128)(2,1)S(1)}, bf16[192,2048]{1,0:T(8,128)(2,1)S(1)}, u32[]{:S(2)}, u32[]{:S(2)}) collective-permute-start(bf16[192,2048]{1,0:T(8,128)(2,1)S(1)} %get-tuple-element.103), channel_id=1, source_target_pairs={{0,1},{1,0},{2,3},{3,2},{4,5},{5,4},{6,7},{7,6},{8,9},{9,8},{10,11... | collective-permute-start | bytes 2359304 | tf_op jit(solution)/shard_map/ppermute | solution.py:206
  145.5 30.2 %copy-start.18 = (bf16[48,2048]{1,0:T(8,128)(2,1)}, bf16[48,2048]{1,0:T(8,128)(2,1)S(1)}, u32[]{:S(2)}) copy-start(bf16[48,2048]{1,0:T(8,128)(2,1)S(1)} %get-tuple-element.90.refs_0_) | copy-start | bytes 589828
  145.5 30.2 %copy-start.14 = (bf16[48,2048]{1,0:T(8,128)(2,1)}, bf16[48,2048]{1,0:T(8,128)(2,1)S(1)}, u32[]{:S(2)}) copy-start(bf16[48,2048]{1,0:T(8,128)(2,1)S(1)} %collective-permute-done.21.refs_6_) | copy-start | bytes 589828
  145.5 7.4 %collective-permute-start.30 = (bf16[48,2048]{1,0:T(8,128)(2,1)S(1)}, bf16[48,2048]{1,0:T(8,128)(2,1)S(1)}, u32[]{:S(2)}, u32[]{:S(2)}) collective-permute-start(bf16[48,2048]{1,0:T(8,128)(2,1)S(1)} %get-tuple-element.91), channel_id=1, source_target_pairs={{0,4},{4,0},{8,12},{12,8},{16,20},{20,16},{24,28},{28,24},{1,5},{5... | collective-permute-start | bytes 589832 | tf_op jit(solution)/shard_map/ppermute | solution.py:206
  147.3 28.4 %copy-start.16 = (bf16[48,2048]{1,0:T(8,128)(2,1)}, bf16[48,2048]{1,0:T(8,128)(2,1)S(1)}, u32[]{:S(2)}) copy-start(bf16[48,2048]{1,0:T(8,128)(2,1)S(1)} %collective-permute-done.22.refs_7_) | copy-start | bytes 589828
  147.3 50.6 %collective-permute-start.43 = (bf16[192,2048]{1,0:T(8,128)(2,1)S(1)}, bf16[192,2048]{1,0:T(8,128)(2,1)S(1)}, u32[]{:S(2)}, u32[]{:S(2)}) collective-permute-start(bf16[192,2048]{1,0:T(8,128)(2,1)S(1)} %get-tuple-element.109), channel_id=1, source_target_pairs={{0,1},{1,0},{2,3},{3,2},{4,5},{5,4},{6,7},{7,6},{8,9},{9,8},{10,11... | collective-permute-start | bytes 2359304 | tf_op jit(solution)/shard_map/ppermute | solution.py:206
  152.9 22.8 %copy-start.20 = (bf16[48,2048]{1,0:T(8,128)(2,1)}, bf16[48,2048]{1,0:T(8,128)(2,1)S(1)}, u32[]{:S(2)}) copy-start(bf16[48,2048]{1,0:T(8,128)(2,1)S(1)} %collective-permute-done.30.refs_1_) | copy-start | bytes 589828
  152.9 6.5 %collective-permute-start.31 = (bf16[48,2048]{1,0:T(8,128)(2,1)S(1)}, bf16[48,2048]{1,0:T(8,128)(2,1)S(1)}, u32[]{:S(2)}, u32[]{:S(2)}) collective-permute-start(bf16[48,2048]{1,0:T(8,128)(2,1)S(1)} %get-tuple-element.92), channel_id=1, source_target_pairs={{0,8},{4,12},{8,0},{12,4},{16,24},{20,28},{24,16},{28,20},{1,9},{5... | collective-permute-start | bytes 589832 | tf_op jit(solution)/shard_map/ppermute | solution.py:206
  159.3 16.4 %copy-start.22 = (bf16[48,2048]{1,0:T(8,128)(2,1)}, bf16[48,2048]{1,0:T(8,128)(2,1)S(1)}, u32[]{:S(2)}) copy-start(bf16[48,2048]{1,0:T(8,128)(2,1)S(1)} %collective-permute-done.31.refs_2_) | copy-start | bytes 589828
  159.3 6.6 %collective-permute-start.32 = (bf16[48,2048]{1,0:T(8,128)(2,1)S(1)}, bf16[48,2048]{1,0:T(8,128)(2,1)S(1)}, u32[]{:S(2)}, u32[]{:S(2)}) collective-permute-start(bf16[48,2048]{1,0:T(8,128)(2,1)S(1)} %get-tuple-element.93), channel_id=1, source_target_pairs={{0,12},{4,8},{8,4},{12,0},{16,28},{20,24},{24,20},{28,16},{1,13},{... | collective-permute-start | bytes 589832 | tf_op jit(solution)/shard_map/ppermute | solution.py:206
  165.9 9.8 %copy-start.24 = (bf16[48,2048]{1,0:T(8,128)(2,1)}, bf16[48,2048]{1,0:T(8,128)(2,1)S(1)}, u32[]{:S(2)}) copy-start(bf16[48,2048]{1,0:T(8,128)(2,1)S(1)} %collective-permute-done.32.refs_3_) | copy-start | bytes 589828
  165.9 22.7 %collective-permute-start.33 = (bf16[48,2048]{1,0:T(8,128)(2,1)S(1)}, bf16[48,2048]{1,0:T(8,128)(2,1)S(1)}, u32[]{:S(2)}, u32[]{:S(2)}) collective-permute-start(bf16[48,2048]{1,0:T(8,128)(2,1)S(1)} %get-tuple-element.94), channel_id=1, source_target_pairs={{0,16},{4,20},{8,24},{12,28},{16,0},{20,4},{24,8},{28,12},{1,17},{... | collective-permute-start | bytes 589832 | tf_op jit(solution)/shard_map/ppermute | solution.py:206
  167.5 26.6 %collective-permute-start.34 = (bf16[48,2048]{1,0:T(8,128)(2,1)S(1)}, bf16[48,2048]{1,0:T(8,128)(2,1)S(1)}, u32[]{:S(2)}, u32[]{:S(2)}) collective-permute-start(bf16[48,2048]{1,0:T(8,128)(2,1)S(1)} %get-tuple-element.95), channel_id=1, source_target_pairs={{0,20},{4,16},{8,28},{12,24},{16,4},{20,0},{24,12},{28,8},{1,21},{... | collective-permute-start | bytes 589832 | tf_op jit(solution)/shard_map/ppermute | solution.py:206
  170.0 24.8 %collective-permute-start.35 = (bf16[48,2048]{1,0:T(8,128)(2,1)S(1)}, bf16[48,2048]{1,0:T(8,128)(2,1)S(1)}, u32[]{:S(2)}, u32[]{:S(2)}) collective-permute-start(bf16[48,2048]{1,0:T(8,128)(2,1)S(1)} %get-tuple-element.96), channel_id=1, source_target_pairs={{0,24},{4,28},{8,16},{12,20},{16,8},{20,12},{24,0},{28,4},{1,25},{... | collective-permute-start | bytes 589832 | tf_op jit(solution)/shard_map/ppermute | solution.py:206
  170.7 26.2 %collective-permute-start.36 = (bf16[48,2048]{1,0:T(8,128)(2,1)S(1)}, bf16[48,2048]{1,0:T(8,128)(2,1)S(1)}, u32[]{:S(2)}, u32[]{:S(2)}) collective-permute-start(bf16[48,2048]{1,0:T(8,128)(2,1)S(1)} %get-tuple-element.97), channel_id=1, source_target_pairs={{0,28},{4,24},{8,20},{12,16},{16,12},{20,8},{24,4},{28,0},{1,29},{... | collective-permute-start | bytes 589832 | tf_op jit(solution)/shard_map/ppermute | solution.py:206
  175.7 23.5 %copy-start.36 = (f32[128,2]{0,1:T(2,128)S(1)}, f32[128,2]{0,1:T(2,128)}, u32[]{:S(2)}) copy-start(f32[128,2]{0,1:T(2,128)} %param.9) | copy-start | bytes 3076
  175.7 23.6 %copy-start.1 = (bf16[128,2048]{1,0:T(8,128)(2,1)S(1)}, bf16[128,2048]{1,0:T(8,128)(2,1)}, u32[]{:S(2)}) copy-start(bf16[128,2048]{1,0:T(8,128)(2,1)} %grad_ref.3) | copy-start | bytes 1572868
  189.3 27.2 %collective-permute-start.45 = (bf16[192,2048]{1,0:T(8,128)(2,1)}, bf16[192,2048]{1,0:T(8,128)(2,1)}, u32[]{:S(2)}, u32[]{:S(2)}) collective-permute-start(bf16[192,2048]{1,0:T(8,128)(2,1)} %shard_map.137), channel_id=1, source_target_pairs={{0,2},{1,3},{2,0},{3,1},{4,6},{5,7},{6,4},{7,5},{8,10},{9,11},{10,... | collective-permute-start | bytes 2359304 | tf_op jit(solution)/shard_map/ppermute | solution.py:206
  194.7 25.3 %collective-permute-start.40 = (bf16[192,2048]{1,0:T(8,128)(2,1)}, bf16[192,2048]{1,0:T(8,128)(2,1)}, u32[]{:S(2)}, u32[]{:S(2)}) collective-permute-start(bf16[192,2048]{1,0:T(8,128)(2,1)} %get-tuple-element.105), channel_id=1, source_target_pairs={{0,1},{1,0},{2,3},{3,2},{4,5},{5,4},{6,7},{7,6},{8,9},{9,8},{10,11... | collective-permute-start | bytes 2359304 | tf_op jit(solution)/shard_map/ppermute | solution.py:206
  195.4 31.5 %collective-permute-start.42 = (bf16[192,2048]{1,0:T(8,128)(2,1)}, bf16[192,2048]{1,0:T(8,128)(2,1)}, u32[]{:S(2)}, u32[]{:S(2)}) collective-permute-start(bf16[192,2048]{1,0:T(8,128)(2,1)} %shard_map.134), channel_id=1, source_target_pairs={{0,2},{1,3},{2,0},{3,1},{4,6},{5,7},{6,4},{7,5},{8,10},{9,11},{10,... | collective-permute-start | bytes 2359304 | tf_op jit(solution)/shard_map/ppermute | solution.py:206
  197.6 31.8 %collective-permute-start.37 = (bf16[192,2048]{1,0:T(8,128)(2,1)}, bf16[192,2048]{1,0:T(8,128)(2,1)}, u32[]{:S(2)}, u32[]{:S(2)}) collective-permute-start(bf16[192,2048]{1,0:T(8,128)(2,1)} %get-tuple-element.101), channel_id=1, source_target_pairs={{0,1},{1,0},{2,3},{3,2},{4,5},{5,4},{6,7},{7,6},{8,9},{9,8},{10,11... | collective-permute-start | bytes 2359304 | tf_op jit(solution)/shard_map/ppermute | solution.py:206
  198.7 43.1 %collective-permute-start.39 = (bf16[192,2048]{1,0:T(8,128)(2,1)}, bf16[192,2048]{1,0:T(8,128)(2,1)}, u32[]{:S(2)}, u32[]{:S(2)}) collective-permute-start(bf16[192,2048]{1,0:T(8,128)(2,1)} %shard_map.131), channel_id=1, source_target_pairs={{0,2},{1,3},{2,0},{3,1},{4,6},{5,7},{6,4},{7,5},{8,10},{9,11},{10,... | collective-permute-start | bytes 2359304 | tf_op jit(solution)/shard_map/ppermute | solution.py:206
  199.4 0.9 copy-start.9
  200.3 0.9 copy-start.11
  201.2 0.9 copy-start.13
  213.4 0.9 copy-start.31
  216.6 1.1 copy-start.6
  (20 other events, 16.0 us)

commit v2 on v1

v2 whole, which is shorter than its diff:
```python
import functools

import jax
import jax.numpy as jnp
from jax import lax
from jax.experimental import pallas as pl
from jax.experimental.pallas import tpu as pltpu
from jax.sharding import PartitionSpec as P


EX, DP = "expert", "dp"
F32 = jnp.float32
BF16 = jnp.bfloat16
VMEM = pl.BlockSpec(memory_space=pltpu.VMEM)
SMEM = pl.BlockSpec(memory_space=pltpu.SMEM)
GRANT = 24 * 1024 * 1024


def silu_parts(preact):
    logistic = jax.nn.sigmoid(preact)
    return (preact * logistic, logistic * (1.0 + preact * (1.0 - logistic)))


def col_tiles(width, step=512):
    step = min(width, step)
    return [slice(n, min(n + step, width)) for n in range(0, width, step)]


def dot_nt(left, right):
    return lax.dot_general(left, right, (((1,), (1,)), ((), ())), preferred_element_type=F32)


def dot_tn(left, right):
    return lax.dot_general(left, right, (((0,), (0,)), ((), ())), preferred_element_type=F32)


def store_chunks(refs, cols, value):
    rows = refs[0].shape[0]
    for r, ref in enumerate(refs):
        ref[:, cols] = value[r * rows : (r + 1) * rows]


def window(ref, part):
    rows = ref.shape[0] if part is None else ref.shape[0] // 2
    return slice(part * rows if part else 0, (part or 0) * rows + rows)


def load_chunks(refs, cols, part=None):
    return jnp.concatenate([ref[window(ref, part), cols] for ref in refs], axis=0)


def load_rows(chunk_refs, rows_ref, part=None, first=0):
    for ref in chunk_refs:
        value = ref[window(ref, part), :]
        rows_ref[first : first + value.shape[0], :] = value
        first += value.shape[0]
    return first


def slots_kernel(experts, capacity, me_ref, ctl_ref, slots_ref):
    routes, toks = slots_ref.shape
    half = experts // 2
    rows = lax.broadcasted_iota(jnp.int32, (experts, toks), 0)
    earlier = (
        lax.broadcasted_iota(jnp.int32, (toks, toks), 0)
        < lax.broadcasted_iota(jnp.int32, (toks, toks), 1)
    ).astype(BF16)
    base = jnp.zeros((experts, 1), F32)
    for k in range(routes):
        rel = ctl_ref[k : k + 1, :].astype(jnp.int32) ^ me_ref[0]
        named = (rows == rel).astype(F32)
        before = jnp.dot(named.astype(BF16), earlier, preferred_element_type=F32) + base
        base = base + jnp.sum(named, axis=1, keepdims=True)
        rank = jnp.sum(before * named, axis=0, keepdims=True).astype(jnp.int32)
        slots_ref[k : k + 1, :] = jnp.where(rel < half, rel * capacity + rank, -1)


def pick(slot, slot_total):
    return lax.broadcasted_iota(jnp.int32, (slot_total, slot.shape[1]), 0) == slot


def as_bf16(hit):
    return hit.astype(F32).astype(BF16)


def as_column(row):
    toks = row.shape[1]
    same = lax.broadcasted_iota(jnp.int32, (toks, toks), 0) == lax.broadcasted_iota(jnp.int32, (toks, toks), 1)
    return jnp.sum(jnp.where(same, row, 0.0), axis=1, keepdims=True)


def as_row(column):
    toks = column.shape[0]
    same = lax.broadcasted_iota(jnp.int32, (toks, toks), 0) == lax.broadcasted_iota(jnp.int32, (toks, toks), 1)
    return jnp.sum(jnp.where(same, column, 0.0), axis=0, keepdims=True)


def chosen_rows(slots_ref, slot_total):
    chosen = None
    for k in range(slots_ref.shape[0]):
        hit = pick(slots_ref[k : k + 1, :], slot_total)
        chosen = hit if chosen is None else chosen | hit
    return as_bf16(chosen)


def send_tokens_kernel(slot_total, slots_ref, tokens_ref, *chunk_refs):
    chosen = chosen_rows(slots_ref, slot_total)
    for cols in col_tiles(tokens_ref.shape[1]):
        rows = jnp.dot(chosen, tokens_ref[:, cols], preferred_element_type=F32)
        store_chunks(chunk_refs, cols, rows.astype(BF16))


def slot_scores(slots_ref, ctl_ref, slot_total):
    routes = slots_ref.shape[0]
    weight = None
    for k in range(routes):
        hit = pick(slots_ref[k : k + 1, :], slot_total)
        score = jnp.where(hit, ctl_ref[routes + k : routes + k + 1, :], 0.0)
        weight = score if weight is None else weight + score
    return jnp.sum(weight, axis=1, keepdims=True)


def send_cots_kernel(slot_total, slots_ref, ctl_ref, grad_ref, *chunk_refs):
    weight = slot_scores(slots_ref, ctl_ref, slot_total)
    chosen = chosen_rows(slots_ref, slot_total)
    for cols in col_tiles(grad_ref.shape[1]):
        rows = jnp.dot(chosen, grad_ref[:, cols], preferred_element_type=F32)
        store_chunks(chunk_refs, cols, (rows * weight).astype(BF16))


def combine_out_kernel(slot_total, n_chunks, part, slots_ref, ctl_ref, grad_ref, *refs):
    chunk_refs, refs = refs[:n_chunks], refs[n_chunks:]
    *came_refs, out_ref, dscore_ref = refs
    routes = slots_ref.shape[0]
    hits, scores = [], []
    for k in range(routes):
        hits.append(as_bf16(pick(slots_ref[k : k + 1, :], slot_total)))
        scores.append(as_column(ctl_ref[routes + k : routes + k + 1, :]))
    dots = [jnp.zeros((grad_ref.shape[0], 1), F32) for _ in range(routes)]
    for cols in col_tiles(grad_ref.shape[1]):
        rows = load_chunks(chunk_refs, cols, part)
        grad = grad_ref[:, cols].astype(F32)
        total = came_refs[0][:, cols].astype(F32) if came_refs else None
        for k in range(routes):
            each = dot_tn(hits[k], rows)
            dots[k] = dots[k] + jnp.sum(each * grad, axis=1, keepdims=True)
            term = scores[k] * each
            total = term if total is None else total + term
        out_ref[:, cols] = total.astype(BF16)
    for k in range(routes):
        dscore = as_row(dots[k])
        if came_refs:
            dscore = dscore + came_refs[1][k : k + 1, :]
        dscore_ref[k : k + 1, :] = dscore


def combine_grad_kernel(slot_total, n_chunks, part, slots_ref, *refs):
    chunk_refs, refs = refs[:n_chunks], refs[n_chunks:]
    *came_refs, out_ref = refs
    chosen = chosen_rows(slots_ref, slot_total)
    for cols in col_tiles(out_ref.shape[1]):
        total = dot_tn(chosen, load_chunks(chunk_refs, cols, part))
        if came_refs:
            total = total + came_refs[0][:, cols].astype(F32)
        out_ref[:, cols] = total.astype(BF16)


def last_kernel(slot_total, n_chunks, first, second, slots_ref, ctl_ref, grad_ref, *refs):
    *refs, out_ref, dscore_ref, token_ref, up_ref = refs
    out_refs, refs = refs[:n_chunks], refs[n_chunks:]
    in_refs = out_refs
    if second is None:
        in_refs, refs = refs[:n_chunks], refs[n_chunks:]
    out_came_ref, dscore_came_ref, grad_came_ref, *up_refs = refs
    add_kernel(*up_refs, up_ref)
    combine_grad_kernel(slot_total, n_chunks, second, slots_ref, *in_refs, grad_came_ref, token_ref)
    combine_out_kernel(
        slot_total, n_chunks, first, slots_ref, ctl_ref, grad_ref, *out_refs, out_came_ref, dscore_came_ref, out_ref, dscore_ref
    )


def expert_in_kernel(n_shards, n_chunks, part, *refs):
    gate_refs, up_refs, refs = refs[:n_shards], refs[n_shards : 2 * n_shards], refs[2 * n_shards :]
    *chunk_refs, gate_ref, up_ref, rows_ref, hidden_ref, act_ref, slope_ref = refs
    load_rows(chunk_refs[n_chunks:], rows_ref, first=load_rows(chunk_refs[:n_chunks], rows_ref, part))
    load_rows(gate_refs, gate_ref)
    load_rows(up_refs, up_ref)
    rows = rows_ref[...]
    for cols in col_tiles(hidden_ref.shape[1], 256):
        gate_pre = dot_nt(rows, gate_ref[cols, :])
        up_pre = dot_nt(rows, up_ref[cols, :])
        activated, slope = silu_parts(gate_pre)
        hidden_ref[:, cols] = (activated * up_pre).astype(BF16)
        act_ref[:, cols] = activated
        slope_ref[:, cols] = slope * up_pre


def expert_out_kernel(n_shards, hidden_ref, *refs):
    shard_refs, down_ref, chunk_refs = refs[:n_shards], refs[n_shards], refs[n_shards + 1 :]
    load_rows(shard_refs, down_ref)
    hidden = hidden_ref[...]
    for cols in col_tiles(down_ref.shape[1]):
        store_chunks(chunk_refs, cols, jnp.dot(hidden, down_ref[:, cols], preferred_element_type=F32).astype(BF16))


def hidden_grad_kernel(down_ref, act_ref, slope_ref, cots_ref, gate_grad_ref, up_grad_ref):
    cots = cots_ref[...]
    for cols in col_tiles(act_ref.shape[1], 256):
        hidden_grad = dot_nt(cots, down_ref[cols, :])
        gate_grad_ref[:, cols] = (hidden_grad * slope_ref[:, cols]).astype(BF16)
        up_grad_ref[:, cols] = (hidden_grad * act_ref[:, cols]).astype(BF16)


def input_grad_kernel(n_chunks, gate_grad_ref, up_grad_ref, gate_ref, up_ref, *refs):
    out_refs, both_refs, pair_refs = refs[: -2 * n_chunks], refs[-2 * n_chunks : -n_chunks], refs[-n_chunks:]
    for out_ref, both_ref in zip(out_refs, both_refs):
        both_ref[window(both_ref, 0), :] = out_ref[...]
    part = 1 if out_refs else None
    gate_grad, up_grad = gate_grad_ref[...], up_grad_ref[...]
    for cols in col_tiles(gate_ref.shape[1]):
        total = jnp.dot(gate_grad, gate_ref[:, cols], preferred_element_type=F32)
        total = total + jnp.dot(up_grad, up_ref[:, cols], preferred_element_type=F32)
        total = total.astype(BF16)
        first = 0
        for ref, where in [(ref, window(ref, part)) for ref in both_refs] + [(ref, window(ref, None)) for ref in pair_refs]:
            count = where.stop - where.start
            ref[where, cols] = total[first : first + count]
            first += count


def weight_grad_kernel(left_ref, right_ref, *part_refs):
    step = part_refs[0].shape[0]
    per = 2 if len(part_refs) % 2 == 0 else len(part_refs)
    for first in range(0, len(part_refs), per):
        left = left_ref[:, first * step : (first + per) * step]
        for cols in col_tiles(right_ref.shape[1]):
            store_chunks(part_refs[first : first + per], cols, dot_tn(left, right_ref[:, cols]).astype(BF16))


def down_grad_kernel(n_chunks, part, hidden_ref, *refs):
    chunk_refs, rows_ref, part_refs = refs[: 2 * n_chunks], refs[2 * n_chunks], refs[2 * n_chunks + 1 :]
    load_rows(chunk_refs[n_chunks:], rows_ref, first=load_rows(chunk_refs[:n_chunks], rows_ref, part))
    weight_grad_kernel(hidden_ref, rows_ref, *part_refs)


def add_kernel(*refs):
    *term_refs, out_ref = refs
    total = term_refs[0][...].astype(F32)
    for ref in term_refs[1:]:
        total = total + ref[...].astype(F32)
    out_ref[...] = total.astype(BF16)


def call(kernel, args, shapes, flops=0):
    single = not isinstance(shapes, list)
    return pl.pallas_call(
        kernel,
        out_shape=shapes,
        in_specs=[SMEM if a.ndim == 1 else VMEM for a in args],
        out_specs=VMEM if single else [VMEM] * len(shapes),
        cost_estimate=pl.CostEstimate(flops=flops, transcendentals=0, bytes_accessed=0),
        compiler_params=pltpu.CompilerParams(vmem_limit_bytes=GRANT),
    )(*args)


def add(terms):
    return call(add_kernel, terms, jax.ShapeDtypeStruct(terms[0].shape, BF16))


def swap(value, axis, bits):
    return lax.ppermute(value, axis, [(i, i ^ bits) for i in range(lax.axis_size(axis))])


def pair_swap(value):
    return swap(value, EX, lax.axis_size(EX) // 2)


def exchange(chunks):
    size = lax.axis_size(EX)
    half = size // 2
    if len(chunks) == 1:
        rows, width = chunks[0].shape
        moved = lax.all_to_all(
            chunks[0].reshape(half, rows // half, width),
            EX,
            split_axis=0,
            concat_axis=0,
            tiled=True,
            axis_index_groups=[list(range(half)), list(range(half, size))],
        )
        return [moved.reshape(rows, width)]
    got = {0: chunks[0]}
    for j in range(half - 1, 0, -1):
        got[j] = swap(chunks[j], EX, j)
    return [got[j] for j in range(half)]


def gather_shards(shard):
    have = {0: shard}
    size = lax.axis_size(DP)
    bit = size // 2
    while bit:
        for j in list(have):
            have[j ^ bit] = swap(have[j], DP, bit)
        bit //= 2
    return [have[j] for j in range(size)]


def scatter_terms(parts):
    terms = {j: [part] for j, part in enumerate(parts)}
    bit = 1
    while bit < len(parts):
        for j in sorted((j for j in terms if j & bit), reverse=True):
            sent = terms.pop(j)
            sent = sent[0] if len(sent) == 1 else add(sent)
            terms[j ^ bit].append(swap(sent, DP, bit))
        bit *= 2
    return terms[0]


def body(tokens, expert_ids, gate_scores, gate_proj, up_proj, down_proj, out_grad):
    tok_count, width = tokens.shape
    routes = expert_ids.shape[1]
    experts = lax.axis_size(EX)
    n_dp = lax.axis_size(DP)
    half = experts // 2
    capacity = max(2, 3 * tok_count * routes // (2 * experts))
    slot_total = half * capacity
    chunked = experts == 8 and capacity % 16 == 0
    n_chunks = half if chunked else 1
    units = gate_proj.shape[1] * n_dp
    flops = 4 * slot_total * width * units

    def shape(rows, cols, dtype=BF16):
        return jax.ShapeDtypeStruct((rows, cols), dtype)

    chunk_shapes = [shape(slot_total // n_chunks, width)] * n_chunks
    both_shapes = [shape(2 * slot_total // n_chunks, width)] * n_chunks
    part_shapes = [shape(units // n_dp, width)] * n_dp
    act_shapes = [shape(2 * slot_total, units)] * 2

    own_ctl = jnp.concatenate([expert_ids.T.astype(F32), gate_scores.T], axis=0)
    pair_ctl = pair_swap(own_ctl)
    pair_tokens = pair_swap(tokens)
    pair_grad = pair_swap(out_grad)
    gate_s = gather_shards(gate_proj[0])
    up_s = gather_shards(up_proj[0])
    down_s = gather_shards(down_proj[0])

    me = lax.axis_index(EX).astype(jnp.int32).reshape(1)
    if not chunked:
        me = me // half * half

    def slots_of(ctl):
        kernel = functools.partial(slots_kernel, experts, capacity)
        return call(kernel, [me, ctl], shape(routes, tok_count, jnp.int32), flops // 100)

    def send_tokens(slots, rows):
        kernel = functools.partial(send_tokens_kernel, slot_total)
        sent = call(kernel, [slots, rows], chunk_shapes, flops // 20)
        return exchange(sent)

    def send_cots(slots, ctl, grad):
        kernel = functools.partial(send_cots_kernel, slot_total)
        sent = call(kernel, [slots, ctl, grad], chunk_shapes, flops // 20)
        return exchange(sent)

    own_slots = slots_of(own_ctl)
    own_tok = send_tokens(own_slots, tokens)
    own_cot = send_cots(own_slots, own_ctl, out_grad)
    pair_slots = slots_of(pair_ctl)
    pair_tok = send_tokens(pair_slots, pair_tokens)
    pair_cot = send_cots(pair_slots, pair_ctl, pair_grad)

    gate_w, up_w, received, hidden, act, slope = call(
        functools.partial(expert_in_kernel, n_dp, n_chunks, None),
        [*gate_s, *up_s, *own_tok, *pair_tok],
        [
            shape(units, width),
            shape(units, width),
            shape(2 * slot_total, width),
            shape(2 * slot_total, units),
            shape(2 * slot_total, units, F32),
            shape(2 * slot_total, units, F32),
        ],
        2 * flops,
    )
    cot_rows, *down_parts = call(
        functools.partial(down_grad_kernel, n_chunks, None),
        [hidden, *own_cot, *pair_cot],
        [shape(2 * slot_total, width)] + part_shapes,
        flops,
    )
    down_w, *out_chunks = call(
        functools.partial(expert_out_kernel, n_dp), [hidden, *down_s], [shape(units, width)] + 2 * chunk_shapes, flops
    )
    pair_out = exchange(out_chunks[n_chunks:])

    def combine_out(part, slots, ctl, grad, *rows):
        return call(
            functools.partial(combine_out_kernel, slot_total, n_chunks, part),
            [slots, ctl, grad, *rows],
            [shape(tok_count, width), shape(routes, tok_count, F32)],
            flops // 10,
        )

    out_part, dscore_part = combine_out(None, pair_slots, pair_ctl, pair_grad, *pair_out)
    out_came = pair_swap(out_part)
    dscore_came = pair_swap(dscore_part)

    gate_grad, up_grad = call(hidden_grad_kernel, [down_w, act, slope, cot_rows], act_shapes, flops)
    gate_parts = call(weight_grad_kernel, [gate_grad, received], part_shapes, flops)
    up_parts = call(weight_grad_kernel, [up_grad, received], part_shapes, flops)
    grad_chunks = call(
        functools.partial(input_grad_kernel, n_chunks),
        [gate_grad, up_grad, gate_w, up_w, *(out_chunks[:n_chunks] if chunked else [])],
        (both_shapes if chunked else chunk_shapes) + chunk_shapes,
        2 * flops,
    )
    own_grad = exchange(grad_chunks[:n_chunks])
    first, second = (0, 1) if chunked else (None, None)
    own_out = own_grad if chunked else exchange(out_chunks[:n_chunks])
    pair_in = exchange(grad_chunks[n_chunks:])

    def combine_grad(part, slots, *rows):
        return call(
            functools.partial(combine_grad_kernel, slot_total, n_chunks, part),
            [slots, *rows],
            shape(tok_count, width),
            flops // 20,
        )

    grad_came = pair_swap(combine_grad(None, pair_slots, *pair_in))

    down_out = add(scatter_terms(down_parts))[None]
    gate_out = add(scatter_terms(gate_parts))[None]
    up_terms = scatter_terms(up_parts)

    own_outs = [shape(tok_count, width), shape(routes, tok_count, F32), shape(tok_count, width), up_terms[0]]
    output, d_scores, d_tokens, up_out = call(
        functools.partial(last_kernel, slot_total, n_chunks, first, second),
        [own_slots, own_ctl, out_grad, *own_out, *(() if chunked else own_grad), out_came, dscore_came, grad_came, *up_terms],
        [jax.ShapeDtypeStruct(a.shape, a.dtype) for a in own_outs],
        flops // 5,
    )
    return (output, d_tokens, d_scores.T, gate_out, up_out[None], down_out)


def solution(mesh):
    rows = P((EX, DP), None)
    weights = P(EX, DP, None)
    return jax.shard_map(
        body,
        mesh=mesh,
        in_specs=(rows, rows, rows, weights, weights, weights, rows),
        out_specs=(rows, rows, rows, weights, weights, weights),
        check_vma=False,
    )
```

time: 245 us -> 211 us (0.86)
  starting transfers between devices: 64.2 us -> 37.9 us
  local copies, waits for them, and re-layouts: 27.4 us -> 1.1 us
  waiting for transfers between devices: 123 us -> 146 us
  Pallas kernels: 29.4 us -> 23.5 us
    unnamed x78 -> x8, local copies, waits for them, and re-layouts: 27.4 us -> 1.1 us
    ppermute x46 -> x45, starting transfers between devices: 64.2 us -> 37.9 us  [swap(): lax.ppermute(value, axis, [(i, i ^ bits) for i in range(lax.axis_size(axi...]
    ppermute x46 -> x45, waiting for transfers between devices: 123 us -> 146 us  [swap(): lax.ppermute(value, axis, [(i, i ^ bits) for i in range(lax.axis_size(axi...]
    pallas_call x21, Pallas kernels: 29.4 us -> 23.5 us  [call(): pl.pallas_call(kernel, out_shape=shapes, in_specs=[SMEM if a.ndim == 1 el...]
  transfers between devices with their start and end apart: 46 -> 45, of which waited for: 18 -> 22; matrix products, arithmetic and copies ran while one was open for 1% -> 1% of each run, Pallas kernels for 9% -> 10%
where the time goes in v2:
time: 211 us
  waiting for transfers between devices  146 us (69%)
  starting transfers between devices  37.9 us (18%)
  Pallas kernels  23.5 us (11%)
    ppermute x45, waiting for transfers between devices, swap(): lax.ppermute(value, axis, [(i, i ^ bits) for i in range(lax.axis_size(axi...  146 us
    ppermute x45, starting transfers between devices, swap(): lax.ppermute(value, axis, [(i, i ^ bits) for i in range(lax.axis_size(axi...  37.9 us
    pallas_call x21, Pallas kernels, call(): pl.pallas_call(kernel, out_shape=shapes, in_specs=[SMEM if a.ndim == 1 el...  23.5 us
  transfers between devices with their start and end apart: 45, of which 22 were waited for; matrix products, arithmetic and copies ran while one was open for 1% of the time, Pallas kernels for 10%

profile of v2, /device:TPU:0, one launch (start us, length us, event | category | flops | bytes accessed | tf_op | source)
XLA Modules:
  0.0 210.6 jit_solution(9699700412187082499)
XLA Ops:
  0.6 4.1 %collective-permute-start.10 = (bf16[128,2048]{1,0:T(8,128)(2,1)}, bf16[128,2048]{1,0:T(8,128)(2,1)S(1)}, u32[]{:S(2)}, u32[]{:S(2)}) collective-permute-start(bf16[128,2048]{1,0:T(8,128)(2,1)} %tokens_ref.1), channel_id=1, source_target_pairs={{0,16},{4,20},{8,24},{12,28},{16,0},{20,4},{24,8},{28,12},{1,17},{... | collective-permute-start | bytes 1572872 | tf_op jit(solution)/shard_map/ppermute | solution.py:271
  4.8 0.7 convert_bitcast_fusion
  5.4 0.7 pad_maximum_fusion.ctl_ref
  6.3 1.0 copy-done
  7.7 1.6 collective-permute-start.6
  9.6 1.6 collective-permute-start.7
  11.3 1.4 shard_map.124
  12.6 15.7 %collective-permute-done.9.ctl_ref = f32[4,128]{1,0:T(4,128)S(1)} collective-permute-done((f32[4,128]{1,0:T(4,128)S(1)}, f32[4,128]{1,0:T(4,128)S(1)}, u32[]{:S(2)}, u32[]{:S(2)}) %collective-permute-start.9) | collective-permute-done | bytes 2080 | tf_op jit(solution)/shard_map/ppermute | solution.py:271
  28.3 1.5 collective-permute-start.17
  29.9 4.0 %collective-permute-start.18 = (bf16[48,2048]{1,0:T(8,128)(2,1)S(1)}, bf16[48,2048]{1,0:T(8,128)(2,1)S(1)}, u32[]{:S(2)}, u32[]{:S(2)}) collective-permute-start(bf16[48,2048]{1,0:T(8,128)(2,1)S(1)} %get-tuple-element.80), channel_id=1, source_target_pairs={{0,8},{4,12},{8,0},{12,4},{16,24},{20,28},{24,16},{28,20},{1,9},{5... | collective-permute-start | bytes 589832 | tf_op jit(solution)/shard_map/ppermute | solution.py:271
  33.9 1.5 collective-permute-start.1
  35.4 0.5 collective-permute-start.4
  36.0 2.4 %collective-permute-start.19 = (bf16[48,2048]{1,0:T(8,128)(2,1)S(1)}, bf16[48,2048]{1,0:T(8,128)(2,1)S(1)}, u32[]{:S(2)}, u32[]{:S(2)}) collective-permute-start(bf16[48,2048]{1,0:T(8,128)(2,1)S(1)} %get-tuple-element.81), channel_id=1, source_target_pairs={{0,12},{4,8},{8,4},{12,0},{16,28},{20,24},{24,20},{28,16},{1,13},{... | collective-permute-start | bytes 589832 | tf_op jit(solution)/shard_map/ppermute | solution.py:271
  38.4 0.4 shard_map.121
  38.8 7.8 %collective-permute-done.18.refs_2_ = bf16[48,2048]{1,0:T(8,128)(2,1)S(1)} collective-permute-done((bf16[48,2048]{1,0:T(8,128)(2,1)S(1)}, bf16[48,2048]{1,0:T(8,128)(2,1)S(1)}, u32[]{:S(2)}, u32[]{:S(2)}) %collective-permute-start.18) | collective-permute-done | bytes 196640 | tf_op jit(solution)/shard_map/ppermute | solution.py:271
  46.6 0.5 collective-permute-start.11
  47.1 1.7 collective-permute-done.19.refs_3_
  48.9 5.8 %collective-permute-done.20.grad_ref = bf16[128,2048]{1,0:T(8,128)(2,1)S(1)} collective-permute-done((bf16[128,2048]{1,0:T(8,128)(2,1)}, bf16[128,2048]{1,0:T(8,128)(2,1)S(1)}, u32[]{:S(2)}, u32[]{:S(2)}) %collective-permute-start.20) | collective-permute-done | bytes 524320 | tf_op jit(solution)/shard_map/ppermute | solution.py:271
  54.7 1.5 collective-permute-start.15
  56.2 6.1 %collective-permute-done.12.refs_14_ = bf16[48,2048]{1,0:T(8,128)(2,1)S(1)} collective-permute-done((bf16[48,2048]{1,0:T(8,128)(2,1)S(1)}, bf16[48,2048]{1,0:T(8,128)(2,1)S(1)}, u32[]{:S(2)}, u32[]{:S(2)}) %collective-permute-start.12) | collective-permute-done | bytes 196640 | tf_op jit(solution)/shard_map/ppermute | solution.py:271
  62.3 6.6 %collective-permute-done.13.refs_15_ = bf16[48,2048]{1,0:T(8,128)(2,1)S(1)} collective-permute-done((bf16[48,2048]{1,0:T(8,128)(2,1)S(1)}, bf16[48,2048]{1,0:T(8,128)(2,1)S(1)}, u32[]{:S(2)}, u32[]{:S(2)}) %collective-permute-start.13) | collective-permute-done | bytes 196640 | tf_op jit(solution)/shard_map/ppermute | solution.py:271
  68.9 0.5 collective-permute-start.2
  69.4 2.0 collective-permute-done.4.refs_6_
  71.4 0.5 collective-permute-start.14
  71.9 14.5 %collective-permute-done.15.refs_2_ = bf16[192,2048]{1,0:T(8,128)(2,1)S(1)} collective-permute-done((bf16[192,2048]{1,0:T(8,128)(2,1)}, bf16[192,2048]{1,0:T(8,128)(2,1)S(1)}, u32[]{:S(2)}, u32[]{:S(2)}) %collective-permute-start.15) | collective-permute-done | bytes 786464 | tf_op jit(solution)/shard_map/ppermute | solution.py:271
  86.8 0.6 collective-permute-start.21
  87.7 2.6 %collective-permute-start.23 = (bf16[48,2048]{1,0:T(8,128)(2,1)S(1)}, bf16[48,2048]{1,0:T(8,128)(2,1)S(1)}, u32[]{:S(2)}, u32[]{:S(2)}) collective-permute-start(bf16[48,2048]{1,0:T(8,128)(2,1)S(1)} %get-tuple-element.85), channel_id=1, source_target_pairs={{0,12},{4,8},{8,4},{12,0},{16,28},{20,24},{24,20},{28,16},{1,13},{... | collective-permute-start | bytes 589832 | tf_op jit(solution)/shard_map/ppermute | solution.py:271
  90.3 2.8 %shard_map.122 = (bf16[768,2048]{1,0:T(8,128)(2,1)S(1)}, bf16[768,2048]{1,0:T(8,128)(2,1)S(1)}, bf16[384,2048]{1,0:T(8,128)(2,1)S(1)}, bf16[384,768]{1,0:T(8,128...) custom-call(bf16[192,2048]{1,0:T(8,128)(2,1)S(1)} %bitcast.13, ...), custom_call_target="tpu_custom_call" | custom-call | flops 2415919104 | tf_op jit(solution)/shard_map/pallas_call | solution.py:256
  93.2 1.0 collective-permute-done.21.refs_5_
  94.2 1.0 collective-permute-done.22.refs_6_
  95.2 4.4 %collective-permute-done.23.refs_7_ = bf16[48,2048]{1,0:T(8,128)(2,1)S(1)} collective-permute-done((bf16[48,2048]{1,0:T(8,128)(2,1)S(1)}, bf16[48,2048]{1,0:T(8,128)(2,1)S(1)}, u32[]{:S(2)}, u32[]{:S(2)}) %collective-permute-start.23) | collective-permute-done | bytes 196640 | tf_op jit(solution)/shard_map/ppermute | solution.py:271
  99.6 1.8 shard_map.126
  101.5 1.4 shard_map.123
  102.9 1.4 shard_map.127
  104.3 2.6 %shard_map.128 = (bf16[96,2048]{1,0:T(8,128)(2,1)S(1)}, bf16[96,2048]{1,0:T(8,128)(2,1)S(1)}, bf16[96,2048]{1,0:T(8,128)(2,1)S(1)}, bf16[96,2048]{1,0:T(8,128)(2...) custom-call(bf16[384,768]{1,0:T(8,128)(2,1)S(1)} %get-tuple-element., ...), custom_call_target="tpu_custom_call" | custom-call | flops 2415919104 | tf_op jit(solution)/shard_map/pallas_call | solution.py:256
  107.0 0.6 collective-permute-start.32
  107.9 1.8 shard_map.134
  109.8 2.7 %collective-permute-start.34 = (bf16[48,2048]{1,0:T(8,128)(2,1)S(1)}, bf16[48,2048]{1,0:T(8,128)(2,1)S(1)}, u32[]{:S(2)}, u32[]{:S(2)}) collective-permute-start(bf16[48,2048]{1,0:T(8,128)(2,1)S(1)} %get-tuple-element.108), channel_id=1, source_target_pairs={{0,12},{4,8},{8,4},{12,0},{16,28},{20,24},{24,20},{28,16},{1,13},{... | collective-permute-start | bytes 589832 | tf_op jit(solution)/shard_map/ppermute | solution.py:271
  112.5 1.8 shard_map.131
  114.5 0.8 collective-permute-done.33.refs_2_
  115.3 1.5 collective-permute-start.27
  116.8 3.0 %collective-permute-done.34.refs_3_ = bf16[48,2048]{1,0:T(8,128)(2,1)S(1)} collective-permute-done((bf16[48,2048]{1,0:T(8,128)(2,1)S(1)}, bf16[48,2048]{1,0:T(8,128)(2,1)S(1)}, u32[]{:S(2)}, u32[]{:S(2)}) %collective-permute-start.34) | collective-permute-done | bytes 196640 | tf_op jit(solution)/shard_map/ppermute | solution.py:271
  120.1 3.8 %collective-permute-done.27.refs_1_ = bf16[48,2048]{1,0:T(8,128)(2,1)S(1)} collective-permute-done((bf16[48,2048]{1,0:T(8,128)(2,1)S(1)}, bf16[48,2048]{1,0:T(8,128)(2,1)S(1)}, u32[]{:S(2)}, u32[]{:S(2)}) %collective-permute-start.27) | collective-permute-done | bytes 196640 | tf_op jit(solution)/shard_map/ppermute | solution.py:271
  123.9 0.9 collective-permute-start.29
  124.8 1.0 collective-permute-done.28.refs_2_
  125.8 0.6 collective-permute-start.24
  126.4 5.3 %collective-permute-done.29.refs_3_ = bf16[48,2048]{1,0:T(8,128)(2,1)S(1)} collective-permute-done((bf16[48,2048]{1,0:T(8,128)(2,1)S(1)}, bf16[48,2048]{1,0:T(8,128)(2,1)S(1)}, u32[]{:S(2)}, u32[]{:S(2)}) %collective-permute-start.29) | collective-permute-done | bytes 196640 | tf_op jit(solution)/shard_map/ppermute | solution.py:271
  131.7 0.6 shard_map.129
  132.4 0.4 collective-permute-start.31
  133.0 3.9 %collective-permute-done.31.refs_5_ = f32[2,128]{1,0:T(2,128)S(1)} collective-permute-done((f32[2,128]{1,0:T(2,128)S(1)}, f32[2,128]{1,0:T(2,128)S(1)}, u32[]{:S(2)}, u32[]{:S(2)}) %collective-permute-start.31) | collective-permute-done | bytes 1056 | tf_op jit(solution)/shard_map/ppermute | solution.py:271
  136.9 1.5 collective-permute-start.44
  138.6 1.2 collective-permute-done.24.refs_1_
  139.8 1.5 collective-permute-start.41
  141.3 0.7 collective-permute-start.25
  142.2 9.7 %collective-permute-done.25.refs_2_ = bf16[96,2048]{1,0:T(8,128)(2,1)S(1)} collective-permute-done((bf16[96,2048]{1,0:T(8,128)(2,1)S(1)}, bf16[96,2048]{1,0:T(8,128)(2,1)S(1)}, u32[]{:S(2)}, u32[]{:S(2)}) %collective-permute-start.25) | collective-permute-done | bytes 393248 | tf_op jit(solution)/shard_map/ppermute | solution.py:271
  151.8 0.5 collective-permute-start.38
  152.7 0.4 collective-permute-start.35
  153.1 4.3 %collective-permute-done.44.refs_2_ = bf16[192,2048]{1,0:T(8,128)(2,1)S(1)} collective-permute-done((bf16[192,2048]{1,0:T(8,128)(2,1)S(1)}, bf16[192,2048]{1,0:T(8,128)(2,1)S(1)}, u32[]{:S(2)}, u32[]{:S(2)}) %collective-permute-start.44) | collective-permute-done | bytes 786464 | tf_op jit(solution)/shard_map/ppermute | solution.py:271
  157.7 16.5 %collective-permute-done.41.refs_2_ = bf16[192,2048]{1,0:T(8,128)(2,1)S(1)} collective-permute-done((bf16[192,2048]{1,0:T(8,128)(2,1)S(1)}, bf16[192,2048]{1,0:T(8,128)(2,1)S(1)}, u32[]{:S(2)}, u32[]{:S(2)}) %collective-permute-start.41) | collective-permute-done | bytes 786464 | tf_op jit(solution)/shard_map/ppermute | solution.py:271
  174.2 0.9 collective-permute-start.26
  175.1 1.2 shard_map.138
  176.3 1.2 shard_map.136
  177.4 29.8 %collective-permute-done.26.refs_3_ = bf16[96,2048]{1,0:T(8,128)(2,1)S(1)} collective-permute-done((bf16[96,2048]{1,0:T(8,128)(2,1)S(1)}, bf16[96,2048]{1,0:T(8,128)(2,1)S(1)}, u32[]{:S(2)}, u32[]{:S(2)}) %collective-permute-start.26) | collective-permute-done | bytes 393248 | tf_op jit(solution)/shard_map/ppermute | solution.py:271
  207.3 3.3 %shard_map.133 = (bf16[128,2048]{1,0:T(8,128)(2,1)}, f32[2,128]{1,0:T(2,128)}, bf16[128,2048]{1,0:T(8,128)(2,1)}, bf16[192,2048]{1,0:T(8,128)(2,1)}) custom-call(s32[2,128]{1,0:T(2,128)S(1)} %shard_map.118.slots_ref, f32[4,128]{1,0:T(4,128)S(1)} %pad_maximum_fusion.ctl_ref, bf16[128,2048]{1,0:T(8,128)(2,1)} %grad_ref.3, ...), custom_call_target="tpu_custom_call" | custom-call | flops 241591904 | tf_op jit(solution)/shard_map/pallas_call | solution.py:256
  (57 shorter events, 4.1 us)
Async XLA Ops:
  0.6 35.3 %collective-permute-start.10 = (bf16[128,2048]{1,0:T(8,128)(2,1)}, bf16[128,2048]{1,0:T(8,128)(2,1)S(1)}, u32[]{:S(2)}, u32[]{:S(2)}) collective-permute-start(bf16[128,2048]{1,0:T(8,128)(2,1)} %tokens_ref.1), channel_id=1, source_target_pairs={{0,16},{4,20},{8,24},{12,28},{16,0},{20,4},{24,8},{28,12},{1,17},{... | collective-permute-start | bytes 1572872 | tf_op jit(solution)/shard_map/ppermute | solution.py:271
  6.2 1.1 copy-start
  7.3 41.6 %copy-start.1 = (bf16[1,192,2048]{2,1,0:T(8,128)(2,1)S(1)}, bf16[1,192,2048]{2,1,0:T(8,128)(2,1)}, u32[]{:S(2)}) copy-start(bf16[1,192,2048]{2,1,0:T(8,128)(2,1)} %param.10) | copy-start | bytes 2359300
  7.3 61.6 %copy-start.2 = (bf16[1,192,2048]{2,1,0:T(8,128)(2,1)S(1)}, bf16[1,192,2048]{2,1,0:T(8,128)(2,1)}, u32[]{:S(2)}) copy-start(bf16[1,192,2048]{2,1,0:T(8,128)(2,1)} %param.11) | copy-start | bytes 2359300
  7.7 22.2 %collective-permute-start.6 = (bf16[48,2048]{1,0:T(8,128)(2,1)S(1)}, bf16[48,2048]{1,0:T(8,128)(2,1)S(1)}, u32[]{:S(2)}, u32[]{:S(2)}) collective-permute-start(bf16[48,2048]{1,0:T(8,128)(2,1)S(1)} %get-tuple-element.67), channel_id=1, source_target_pairs={{0,4},{4,0},{8,12},{12,8},{16,20},{20,16},{24,28},{28,24},{1,5},{5... | collective-permute-start | bytes 589832 | tf_op jit(solution)/shard_map/ppermute | solution.py:271
  9.2 19.1 %collective-permute-start.9 = (f32[4,128]{1,0:T(4,128)S(1)}, f32[4,128]{1,0:T(4,128)S(1)}, u32[]{:S(2)}, u32[]{:S(2)}) collective-permute-start(f32[4,128]{1,0:T(4,128)S(1)} %pad_maximum_fusion.ctl_ref), channel_id=1, source_target_pairs={{0,16},{4,20},{8,24},{12,28},{16,0},{20,4},{24,8},{28,12},{1,17},{... | collective-permute-start | bytes 6152 | tf_op jit(solution)/shard_map/ppermute | solution.py:271
  9.6 20.3 %collective-permute-start.7 = (bf16[48,2048]{1,0:T(8,128)(2,1)S(1)}, bf16[48,2048]{1,0:T(8,128)(2,1)S(1)}, u32[]{:S(2)}, u32[]{:S(2)}) collective-permute-start(bf16[48,2048]{1,0:T(8,128)(2,1)S(1)} %get-tuple-element.68), channel_id=1, source_target_pairs={{0,8},{4,12},{8,0},{12,4},{16,24},{20,28},{24,16},{28,20},{1,9},{5... | collective-permute-start | bytes 589832 | tf_op jit(solution)/shard_map/ppermute | solution.py:271
  11.1 22.8 %collective-permute-start.8 = (bf16[48,2048]{1,0:T(8,128)(2,1)S(1)}, bf16[48,2048]{1,0:T(8,128)(2,1)S(1)}, u32[]{:S(2)}, u32[]{:S(2)}) collective-permute-start(bf16[48,2048]{1,0:T(8,128)(2,1)S(1)} %get-tuple-element.69), channel_id=1, source_target_pairs={{0,12},{4,8},{8,4},{12,0},{16,28},{20,24},{24,20},{28,16},{1,13},{... | collective-permute-start | bytes 589832 | tf_op jit(solution)/shard_map/ppermute | solution.py:271
  28.3 7.1 %collective-permute-start.17 = (bf16[48,2048]{1,0:T(8,128)(2,1)S(1)}, bf16[48,2048]{1,0:T(8,128)(2,1)S(1)}, u32[]{:S(2)}, u32[]{:S(2)}) collective-permute-start(bf16[48,2048]{1,0:T(8,128)(2,1)S(1)} %get-tuple-element.79), channel_id=1, source_target_pairs={{0,4},{4,0},{8,12},{12,8},{16,20},{20,16},{24,28},{28,24},{1,5},{5... | collective-permute-start | bytes 589832 | tf_op jit(solution)/shard_map/ppermute | solution.py:271
  29.9 24.8 %collective-permute-start.20 = (bf16[128,2048]{1,0:T(8,128)(2,1)}, bf16[128,2048]{1,0:T(8,128)(2,1)S(1)}, u32[]{:S(2)}, u32[]{:S(2)}) collective-permute-start(bf16[128,2048]{1,0:T(8,128)(2,1)} %grad_ref.3), channel_id=1, source_target_pairs={{0,16},{4,20},{8,24},{12,28},{16,0},{20,4},{24,8},{28,12},{1,17},{... | collective-permute-start | bytes 1572872 | tf_op jit(solution)/shard_map/ppermute | solution.py:271
  29.9 16.8 %collective-permute-start.18 = (bf16[48,2048]{1,0:T(8,128)(2,1)S(1)}, bf16[48,2048]{1,0:T(8,128)(2,1)S(1)}, u32[]{:S(2)}, u32[]{:S(2)}) collective-permute-start(bf16[48,2048]{1,0:T(8,128)(2,1)S(1)} %get-tuple-element.80), channel_id=1, source_target_pairs={{0,8},{4,12},{8,0},{12,4},{16,24},{20,28},{24,16},{28,20},{1,9},{5... | collective-permute-start | bytes 589832 | tf_op jit(solution)/shard_map/ppermute | solution.py:271
  33.9 35.0 %collective-permute-start.1 = (bf16[192,2048]{1,0:T(8,128)(2,1)}, bf16[192,2048]{1,0:T(8,128)(2,1)S(1)}, u32[]{:S(2)}, u32[]{:S(2)}) collective-permute-start(bf16[192,2048]{1,0:T(8,128)(2,1)} %bitcast.11), channel_id=1, source_target_pairs={{0,2},{1,3},{2,0},{3,1},{4,6},{5,7},{6,4},{7,5},{8,10},{9,11},{10,... | collective-permute-start | bytes 2359304 | tf_op jit(solution)/shard_map/ppermute | solution.py:271
  35.4 36.0 %collective-permute-start.4 = (bf16[192,2048]{1,0:T(8,128)(2,1)}, bf16[192,2048]{1,0:T(8,128)(2,1)S(1)}, u32[]{:S(2)}, u32[]{:S(2)}) collective-permute-start(bf16[192,2048]{1,0:T(8,128)(2,1)} %bitcast.14), channel_id=1, source_target_pairs={{0,2},{1,3},{2,0},{3,1},{4,6},{5,7},{6,4},{7,5},{8,10},{9,11},{10,... | collective-permute-start | bytes 2359304 | tf_op jit(solution)/shard_map/ppermute | solution.py:271
  36.0 12.9 %collective-permute-start.19 = (bf16[48,2048]{1,0:T(8,128)(2,1)S(1)}, bf16[48,2048]{1,0:T(8,128)(2,1)S(1)}, u32[]{:S(2)}, u32[]{:S(2)}) collective-permute-start(bf16[48,2048]{1,0:T(8,128)(2,1)S(1)} %get-tuple-element.81), channel_id=1, source_target_pairs={{0,12},{4,8},{8,4},{12,0},{16,28},{20,24},{24,20},{28,16},{1,13},{... | collective-permute-start | bytes 589832 | tf_op jit(solution)/shard_map/ppermute | solution.py:271
  46.6 9.6 %collective-permute-start.11 = (bf16[48,2048]{1,0:T(8,128)(2,1)S(1)}, bf16[48,2048]{1,0:T(8,128)(2,1)S(1)}, u32[]{:S(2)}, u32[]{:S(2)}) collective-permute-start(bf16[48,2048]{1,0:T(8,128)(2,1)S(1)} %get-tuple-element.71), channel_id=1, source_target_pairs={{0,4},{4,0},{8,12},{12,8},{16,20},{20,16},{24,28},{28,24},{1,5},{5... | collective-permute-start | bytes 589832 | tf_op jit(solution)/shard_map/ppermute | solution.py:271
  48.9 22.5 %collective-permute-start = (bf16[192,2048]{1,0:T(8,128)(2,1)S(1)}, bf16[192,2048]{1,0:T(8,128)(2,1)S(1)}, u32[]{:S(2)}, u32[]{:S(2)}) collective-permute-start(bf16[192,2048]{1,0:T(8,128)(2,1)S(1)} %bitcast.12), channel_id=1, source_target_pairs={{0,1},{1,0},{2,3},{3,2},{4,5},{5,4},{6,7},{7,6},{8,9},{9,8},{10,11... | collective-permute-start | bytes 2359304 | tf_op jit(solution)/shard_map/ppermute | solution.py:271
  54.7 31.7 %collective-permute-start.15 = (bf16[192,2048]{1,0:T(8,128)(2,1)}, bf16[192,2048]{1,0:T(8,128)(2,1)S(1)}, u32[]{:S(2)}, u32[]{:S(2)}) collective-permute-start(bf16[192,2048]{1,0:T(8,128)(2,1)} %bitcast.17), channel_id=1, source_target_pairs={{0,2},{1,3},{2,0},{3,1},{4,6},{5,7},{6,4},{7,5},{8,10},{9,11},{10,... | collective-permute-start | bytes 2359304 | tf_op jit(solution)/shard_map/ppermute | solution.py:271
  56.2 6.1 %collective-permute-start.12 = (bf16[48,2048]{1,0:T(8,128)(2,1)S(1)}, bf16[48,2048]{1,0:T(8,128)(2,1)S(1)}, u32[]{:S(2)}, u32[]{:S(2)}) collective-permute-start(bf16[48,2048]{1,0:T(8,128)(2,1)S(1)} %get-tuple-element.72), channel_id=1, source_target_pairs={{0,8},{4,12},{8,0},{12,4},{16,24},{20,28},{24,16},{28,20},{1,9},{5... | collective-permute-start | bytes 589832 | tf_op jit(solution)/shard_map/ppermute | solution.py:271
  62.3 6.6 %collective-permute-start.13 = (bf16[48,2048]{1,0:T(8,128)(2,1)S(1)}, bf16[48,2048]{1,0:T(8,128)(2,1)S(1)}, u32[]{:S(2)}, u32[]{:S(2)}) collective-permute-start(bf16[48,2048]{1,0:T(8,128)(2,1)S(1)} %get-tuple-element.73), channel_id=1, source_target_pairs={{0,12},{4,8},{8,4},{12,0},{16,28},{20,24},{24,20},{28,16},{1,13},{... | collective-permute-start | bytes 589832 | tf_op jit(solution)/shard_map/ppermute | solution.py:271
  68.9 17.9 %collective-permute-start.3 = (bf16[192,2048]{1,0:T(8,128)(2,1)S(1)}, bf16[192,2048]{1,0:T(8,128)(2,1)S(1)}, u32[]{:S(2)}, u32[]{:S(2)}) collective-permute-start(bf16[192,2048]{1,0:T(8,128)(2,1)S(1)} %bitcast.15), channel_id=1, source_target_pairs={{0,1},{1,0},{2,3},{3,2},{4,5},{5,4},{6,7},{7,6},{8,9},{9,8},{10,11... | collective-permute-start | bytes 2359304 | tf_op jit(solution)/shard_map/ppermute | solution.py:271
  68.9 18.5 %collective-permute-start.2 = (bf16[192,2048]{1,0:T(8,128)(2,1)S(1)}, bf16[192,2048]{1,0:T(8,128)(2,1)S(1)}, u32[]{:S(2)}, u32[]{:S(2)}) collective-permute-start(bf16[192,2048]{1,0:T(8,128)(2,1)S(1)} %collective-permute-done.1.refs_2_), channel_id=1, source_target_pairs={{0,1},{1,0},{2,3},{3,2},{4,5},{5,4},{6,7},{7,6},{8,9},{9,8},{10,11... | collective-permute-start | bytes 2359304 | tf_op jit(solution)/shard_map/ppermute | solution.py:271
  71.4 16.3 %collective-permute-start.5 = (bf16[192,2048]{1,0:T(8,128)(2,1)S(1)}, bf16[192,2048]{1,0:T(8,128)(2,1)S(1)}, u32[]{:S(2)}, u32[]{:S(2)}) collective-permute-start(bf16[192,2048]{1,0:T(8,128)(2,1)S(1)} %collective-permute-done.4.refs_6_), channel_id=1, source_target_pairs={{0,1},{1,0},{2,3},{3,2},{4,5},{5,4},{6,7},{7,6},{8,9},{9,8},{10,11... | collective-permute-start | bytes 2359304 | tf_op jit(solution)/shard_map/ppermute | solution.py:271
  71.4 30.1 %collective-permute-start.14 = (bf16[192,2048]{1,0:T(8,128)(2,1)}, bf16[192,2048]{1,0:T(8,128)(2,1)S(1)}, u32[]{:S(2)}, u32[]{:S(2)}) collective-permute-start(bf16[192,2048]{1,0:T(8,128)(2,1)} %bitcast.18), channel_id=1, source_target_pairs={{0,1},{1,0},{2,3},{3,2},{4,5},{5,4},{6,7},{7,6},{8,9},{9,8},{10,11... | collective-permute-start | bytes 2359304 | tf_op jit(solution)/shard_map/ppermute | solution.py:271
  86.4 15.1 %collective-permute-start.16 = (bf16[192,2048]{1,0:T(8,128)(2,1)S(1)}, bf16[192,2048]{1,0:T(8,128)(2,1)S(1)}, u32[]{:S(2)}, u32[]{:S(2)}) collective-permute-start(bf16[192,2048]{1,0:T(8,128)(2,1)S(1)} %collective-permute-done.15.refs_2_), channel_id=1, source_target_pairs={{0,1},{1,0},{2,3},{3,2},{4,5},{5,4},{6,7},{7,6},{8,9},{9,8},{10,11... | collective-permute-start | bytes 2359304 | tf_op jit(solution)/shard_map/ppermute | solution.py:271
  86.8 7.4 %collective-permute-start.21 = (bf16[48,2048]{1,0:T(8,128)(2,1)S(1)}, bf16[48,2048]{1,0:T(8,128)(2,1)S(1)}, u32[]{:S(2)}, u32[]{:S(2)}) collective-permute-start(bf16[48,2048]{1,0:T(8,128)(2,1)S(1)} %get-tuple-element.83), channel_id=1, source_target_pairs={{0,4},{4,0},{8,12},{12,8},{16,20},{20,16},{24,28},{28,24},{1,5},{5... | collective-permute-start | bytes 589832 | tf_op jit(solution)/shard_map/ppermute | solution.py:271
  87.4 7.8 %collective-permute-start.22 = (bf16[48,2048]{1,0:T(8,128)(2,1)S(1)}, bf16[48,2048]{1,0:T(8,128)(2,1)S(1)}, u32[]{:S(2)}, u32[]{:S(2)}) collective-permute-start(bf16[48,2048]{1,0:T(8,128)(2,1)S(1)} %get-tuple-element.84), channel_id=1, source_target_pairs={{0,8},{4,12},{8,0},{12,4},{16,24},{20,28},{24,16},{28,20},{1,9},{5... | collective-permute-start | bytes 589832 | tf_op jit(solution)/shard_map/ppermute | solution.py:271
  87.7 11.8 %collective-permute-start.23 = (bf16[48,2048]{1,0:T(8,128)(2,1)S(1)}, bf16[48,2048]{1,0:T(8,128)(2,1)S(1)}, u32[]{:S(2)}, u32[]{:S(2)}) collective-permute-start(bf16[48,2048]{1,0:T(8,128)(2,1)S(1)} %get-tuple-element.85), channel_id=1, source_target_pairs={{0,12},{4,8},{8,4},{12,0},{16,28},{20,24},{24,20},{28,16},{1,13},{... | collective-permute-start | bytes 589832 | tf_op jit(solution)/shard_map/ppermute | solution.py:271
  99.6 1.9 copy-start.3
  101.4 31.0 %collective-permute-start.43 = (bf16[192,2048]{1,0:T(8,128)(2,1)S(1)}, bf16[192,2048]{1,0:T(8,128)(2,1)S(1)}, u32[]{:S(2)}, u32[]{:S(2)}) collective-permute-start(bf16[192,2048]{1,0:T(8,128)(2,1)S(1)} %get-tuple-element.125), channel_id=1, source_target_pairs={{0,1},{1,0},{2,3},{3,2},{4,5},{5,4},{6,7},{7,6},{8,9},{9,8},{10,11... | collective-permute-start | bytes 2359304 | tf_op jit(solution)/shard_map/ppermute | solution.py:271
  107.0 7.3 %collective-permute-start.32 = (bf16[48,2048]{1,0:T(8,128)(2,1)S(1)}, bf16[48,2048]{1,0:T(8,128)(2,1)S(1)}, u32[]{:S(2)}, u32[]{:S(2)}) collective-permute-start(bf16[48,2048]{1,0:T(8,128)(2,1)S(1)} %get-tuple-element.106), channel_id=1, source_target_pairs={{0,4},{4,0},{8,12},{12,8},{16,20},{20,16},{24,28},{28,24},{1,5},{5... | collective-permute-start | bytes 589832 | tf_op jit(solution)/shard_map/ppermute | solution.py:271
  107.6 7.8 %collective-permute-start.33 = (bf16[48,2048]{1,0:T(8,128)(2,1)S(1)}, bf16[48,2048]{1,0:T(8,128)(2,1)S(1)}, u32[]{:S(2)}, u32[]{:S(2)}) collective-permute-start(bf16[48,2048]{1,0:T(8,128)(2,1)S(1)} %get-tuple-element.107), channel_id=1, source_target_pairs={{0,8},{4,12},{8,0},{12,4},{16,24},{20,28},{24,16},{28,20},{1,9},{5... | collective-permute-start | bytes 589832 | tf_op jit(solution)/shard_map/ppermute | solution.py:271
  109.7 27.2 %collective-permute-start.40 = (bf16[192,2048]{1,0:T(8,128)(2,1)S(1)}, bf16[192,2048]{1,0:T(8,128)(2,1)S(1)}, u32[]{:S(2)}, u32[]{:S(2)}) collective-permute-start(bf16[192,2048]{1,0:T(8,128)(2,1)S(1)} %get-tuple-element.120), channel_id=1, source_target_pairs={{0,1},{1,0},{2,3},{3,2},{4,5},{5,4},{6,7},{7,6},{8,9},{9,8},{10,11... | collective-permute-start | bytes 2359304 | tf_op jit(solution)/shard_map/ppermute | solution.py:271
  109.8 10.0 %collective-permute-start.34 = (bf16[48,2048]{1,0:T(8,128)(2,1)S(1)}, bf16[48,2048]{1,0:T(8,128)(2,1)S(1)}, u32[]{:S(2)}, u32[]{:S(2)}) collective-permute-start(bf16[48,2048]{1,0:T(8,128)(2,1)S(1)} %get-tuple-element.108), channel_id=1, source_target_pairs={{0,12},{4,8},{8,4},{12,0},{16,28},{20,24},{24,20},{28,16},{1,13},{... | collective-permute-start | bytes 589832 | tf_op jit(solution)/shard_map/ppermute | solution.py:271
  114.3 27.0 %collective-permute-start.37 = (bf16[192,2048]{1,0:T(8,128)(2,1)S(1)}, bf16[192,2048]{1,0:T(8,128)(2,1)S(1)}, u32[]{:S(2)}, u32[]{:S(2)}) collective-permute-start(bf16[192,2048]{1,0:T(8,128)(2,1)S(1)} %get-tuple-element.113), channel_id=1, source_target_pairs={{0,1},{1,0},{2,3},{3,2},{4,5},{5,4},{6,7},{7,6},{8,9},{9,8},{10,11... | collective-permute-start | bytes 2359304 | tf_op jit(solution)/shard_map/ppermute | solution.py:271
  115.3 8.6 %collective-permute-start.27 = (bf16[48,2048]{1,0:T(8,128)(2,1)S(1)}, bf16[48,2048]{1,0:T(8,128)(2,1)S(1)}, u32[]{:S(2)}, u32[]{:S(2)}) collective-permute-start(bf16[48,2048]{1,0:T(8,128)(2,1)S(1)} %get-tuple-element.100), channel_id=1, source_target_pairs={{0,4},{4,0},{8,12},{12,8},{16,20},{20,16},{24,28},{28,24},{1,5},{5... | collective-permute-start | bytes 589832 | tf_op jit(solution)/shard_map/ppermute | solution.py:271
  119.8 6.0 %collective-permute-start.28 = (bf16[48,2048]{1,0:T(8,128)(2,1)S(1)}, bf16[48,2048]{1,0:T(8,128)(2,1)S(1)}, u32[]{:S(2)}, u32[]{:S(2)}) collective-permute-start(bf16[48,2048]{1,0:T(8,128)(2,1)S(1)} %get-tuple-element.101), channel_id=1, source_target_pairs={{0,8},{4,12},{8,0},{12,4},{16,24},{20,28},{24,16},{28,20},{1,9},{5... | collective-permute-start | bytes 589832 | tf_op jit(solution)/shard_map/ppermute | solution.py:271
  123.9 7.8 %collective-permute-start.29 = (bf16[48,2048]{1,0:T(8,128)(2,1)S(1)}, bf16[48,2048]{1,0:T(8,128)(2,1)S(1)}, u32[]{:S(2)}, u32[]{:S(2)}) collective-permute-start(bf16[48,2048]{1,0:T(8,128)(2,1)S(1)} %get-tuple-element.102), channel_id=1, source_target_pairs={{0,12},{4,8},{8,4},{12,0},{16,28},{20,24},{24,20},{28,16},{1,13},{... | collective-permute-start | bytes 589832 | tf_op jit(solution)/shard_map/ppermute | solution.py:271
  125.8 14.0 %collective-permute-start.24 = (bf16[96,2048]{1,0:T(8,128)(2,1)S(1)}, bf16[96,2048]{1,0:T(8,128)(2,1)S(1)}, u32[]{:S(2)}, u32[]{:S(2)}) collective-permute-start(bf16[96,2048]{1,0:T(8,128)(2,1)S(1)} %get-tuple-element.96), channel_id=1, source_target_pairs={{0,4},{4,0},{8,12},{12,8},{16,20},{20,16},{24,28},{28,24},{1,5},{5... | collective-permute-start | bytes 1179656 | tf_op jit(solution)/shard_map/ppermute | solution.py:271
  131.7 20.1 %collective-permute-start.42 = (bf16[192,2048]{1,0:T(8,128)(2,1)S(1)}, bf16[192,2048]{1,0:T(8,128)(2,1)S(1)}, u32[]{:S(2)}, u32[]{:S(2)}) collective-permute-start(bf16[192,2048]{1,0:T(8,128)(2,1)S(1)} %get-tuple-element.123), channel_id=1, source_target_pairs={{0,1},{1,0},{2,3},{3,2},{4,5},{5,4},{6,7},{7,6},{8,9},{9,8},{10,11... | collective-permute-start | bytes 2359304 | tf_op jit(solution)/shard_map/ppermute | solution.py:271
  132.4 4.5 %collective-permute-start.31 = (f32[2,128]{1,0:T(2,128)S(1)}, f32[2,128]{1,0:T(2,128)S(1)}, u32[]{:S(2)}, u32[]{:S(2)}) collective-permute-start(f32[2,128]{1,0:T(2,128)S(1)} %get-tuple-element.104), channel_id=1, source_target_pairs={{0,16},{4,20},{8,24},{12,28},{16,0},{20,4},{24,8},{28,12},{1,17},{... | collective-permute-start | bytes 3080 | tf_op jit(solution)/shard_map/ppermute | solution.py:271
  136.9 15.7 %collective-permute-start.39 = (bf16[192,2048]{1,0:T(8,128)(2,1)S(1)}, bf16[192,2048]{1,0:T(8,128)(2,1)S(1)}, u32[]{:S(2)}, u32[]{:S(2)}) collective-permute-start(bf16[192,2048]{1,0:T(8,128)(2,1)S(1)} %get-tuple-element.118), channel_id=1, source_target_pairs={{0,1},{1,0},{2,3},{3,2},{4,5},{5,4},{6,7},{7,6},{8,9},{9,8},{10,11... | collective-permute-start | bytes 2359304 | tf_op jit(solution)/shard_map/ppermute | solution.py:271
  136.9 20.4 %collective-permute-start.44 = (bf16[192,2048]{1,0:T(8,128)(2,1)S(1)}, bf16[192,2048]{1,0:T(8,128)(2,1)S(1)}, u32[]{:S(2)}, u32[]{:S(2)}) collective-permute-start(bf16[192,2048]{1,0:T(8,128)(2,1)S(1)} %shard_map.137), channel_id=1, source_target_pairs={{0,2},{1,3},{2,0},{3,1},{4,6},{5,7},{6,4},{7,5},{8,10},{9,11},{10,... | collective-permute-start | bytes 2359304 | tf_op jit(solution)/shard_map/ppermute | solution.py:271
  139.8 34.4 %collective-permute-start.41 = (bf16[192,2048]{1,0:T(8,128)(2,1)S(1)}, bf16[192,2048]{1,0:T(8,128)(2,1)S(1)}, u32[]{:S(2)}, u32[]{:S(2)}) collective-permute-start(bf16[192,2048]{1,0:T(8,128)(2,1)S(1)} %shard_map.135), channel_id=1, source_target_pairs={{0,2},{1,3},{2,0},{3,1},{4,6},{5,7},{6,4},{7,5},{8,10},{9,11},{10,... | collective-permute-start | bytes 2359304 | tf_op jit(solution)/shard_map/ppermute | solution.py:271
  141.3 10.5 %collective-permute-start.25 = (bf16[96,2048]{1,0:T(8,128)(2,1)S(1)}, bf16[96,2048]{1,0:T(8,128)(2,1)S(1)}, u32[]{:S(2)}, u32[]{:S(2)}) collective-permute-start(bf16[96,2048]{1,0:T(8,128)(2,1)S(1)} %get-tuple-element.97), channel_id=1, source_target_pairs={{0,8},{4,12},{8,0},{12,4},{16,24},{20,28},{24,16},{28,20},{1,9},{5... | collective-permute-start | bytes 1179656 | tf_op jit(solution)/shard_map/ppermute | solution.py:271
  151.8 55.5 %collective-permute-start.36 = (bf16[192,2048]{1,0:T(8,128)(2,1)S(1)}, bf16[192,2048]{1,0:T(8,128)(2,1)S(1)}, u32[]{:S(2)}, u32[]{:S(2)}) collective-permute-start(bf16[192,2048]{1,0:T(8,128)(2,1)S(1)} %get-tuple-element.111), channel_id=1, source_target_pairs={{0,1},{1,0},{2,3},{3,2},{4,5},{5,4},{6,7},{7,6},{8,9},{9,8},{10,11... | collective-permute-start | bytes 2359304 | tf_op jit(solution)/shard_map/ppermute | solution.py:271
  151.8 55.5 %collective-permute-start.38 = (bf16[192,2048]{1,0:T(8,128)(2,1)S(1)}, bf16[192,2048]{1,0:T(8,128)(2,1)S(1)}, u32[]{:S(2)}, u32[]{:S(2)}) collective-permute-start(bf16[192,2048]{1,0:T(8,128)(2,1)S(1)} %shard_map.132), channel_id=1, source_target_pairs={{0,2},{1,3},{2,0},{3,1},{4,6},{5,7},{6,4},{7,5},{8,10},{9,11},{10,... | collective-permute-start | bytes 2359304 | tf_op jit(solution)/shard_map/ppermute | solution.py:271
  152.7 54.6 %collective-permute-start.35 = (bf16[128,2048]{1,0:T(8,128)(2,1)S(1)}, bf16[128,2048]{1,0:T(8,128)(2,1)S(1)}, u32[]{:S(2)}, u32[]{:S(2)}) collective-permute-start(bf16[128,2048]{1,0:T(8,128)(2,1)S(1)} %shard_map.130), channel_id=1, source_target_pairs={{0,16},{4,20},{8,24},{12,28},{16,0},{20,4},{24,8},{28,12},{1,17},{... | collective-permute-start | bytes 1572872 | tf_op jit(solution)/shard_map/ppermute | solution.py:271
  157.3 49.9 %collective-permute-start.30 = (bf16[128,2048]{1,0:T(8,128)(2,1)S(1)}, bf16[128,2048]{1,0:T(8,128)(2,1)S(1)}, u32[]{:S(2)}, u32[]{:S(2)}) collective-permute-start(bf16[128,2048]{1,0:T(8,128)(2,1)S(1)} %get-tuple-element.103), channel_id=1, source_target_pairs={{0,16},{4,20},{8,24},{12,28},{16,0},{20,4},{24,8},{28,12},{1,17},{... | collective-permute-start | bytes 1572872 | tf_op jit(solution)/shard_map/ppermute | solution.py:271
  174.2 33.1 %collective-permute-start.26 = (bf16[96,2048]{1,0:T(8,128)(2,1)S(1)}, bf16[96,2048]{1,0:T(8,128)(2,1)S(1)}, u32[]{:S(2)}, u32[]{:S(2)}) collective-permute-start(bf16[96,2048]{1,0:T(8,128)(2,1)S(1)} %get-tuple-element.98), channel_id=1, source_target_pairs={{0,12},{4,8},{8,4},{12,0},{16,28},{20,24},{24,20},{28,16},{1,13},{... | collective-permute-start | bytes 1179656 | tf_op jit(solution)/shard_map/ppermute | solution.py:271
